TPU v7x, 512 devices: a whole 4x8x8 slice. The times are simulated.
512 devices in a mesh: dap: 128 (over z, y_lo, x, core), seq: 4 (over y_hi).
Axes of the slice: x: 4, y: 8 (y_hi: 4, y_lo: 2; y = y_hi * 2 + y_lo), z: 8, core: 2. Of those that a mesh axis runs over, the one named last changes fastest.
Arguments:
- homolog_tensor: bfloat16 [128, 512, 256], P('dap', 'seq'), may hold values from -6 to 6
- pair_features: bfloat16 [512, 512, 128], P('seq', 'dap'), may hold values from -6 to 6
- entry_real_mask: int32 [128, 512], P('dap', 'seq'), may hold values 0 or 1
- chain_ids: int32 [512], replicated, may hold values from 0 to 3, never falling along the last dimension, each value on 1 to 256 neighbouring positions
- horizontal_matrices: bfloat16 [256, 1024], replicated, may hold values from -0.375 to 0.375
- horizontal_projector: bfloat16 [256, 256], replicated, may hold values from -0.375 to 0.375
- bias_proj: float32 [128, 8], replicated, may hold values from -35.35534 to 35.35534
- chain_bias: float32 [2, 8], replicated, may hold values from -4 to 4
- column_proj: bfloat16 [256, 1024], replicated, may hold values from -12.5 to 12.5
- vertical_projector: bfloat16 [256, 256], replicated, may hold values from -0.375 to 0.375
- expansion_matrix: bfloat16 [256, 1024], replicated, may hold values from -0.375 to 0.375
- contraction_matrix: bfloat16 [1024, 256], replicated, may hold values from -0.1875 to 0.1875
Outputs:
- updated: bfloat16 [128, 512, 256], P('dap', 'seq')
Inputs may be any that keep to these rules, and one draw needn't show every extreme that they name: `chain_ids`: chain numbers never fall along the residues.
All inputs are finite; a program needn't handle non-finite values. No bound on the sum of `entry_real_mask` on one device may be relied on, other than what follows from the above.
Results may differ from a plain program's by a relative error of at most 0.013.
The roundings to bfloat16 on the way count: a program that leaves them out, or rounds other values in their place, can miss the bound.
Values may be sent and summed in bfloat16 or wider, within the bound.
A program may use at most 64 MiB of HBM per device.

v0:
```python
import math

import jax
import jax.numpy as jnp
from jax import lax
from jax.sharding import Mesh
from jax.sharding import PartitionSpec as P

HEAD_TOTAL = 8
HEAD_DEPTH = 32
DAP = ("dap_0", "dap_1", "dap_2", "dap_3")


epsilon = 1e-05


def sent_to_all(shard, axis):
    copies = jnp.broadcast_to(shard, (lax.axis_size(axis), *shard.shape))
    return lax.all_to_all(copies, axis, split_axis=0, concat_axis=0, tiled=True)


def in_order(tiles, dim):
    lengths = list(tiles.shape[1:])
    lengths[dim] *= tiles.shape[0]
    return jnp.moveaxis(tiles, 0, dim).reshape(lengths)


def whole_of(shard, axes, dim):
    far, near = axes
    tiles = sent_to_all(sent_to_all(shard, far), near)
    return in_order(tiles.swapaxes(0, 1).reshape(-1, *shard.shape), dim)


def side_by_side(arrays, axis, dim, along):
    widths = [math.prod(a.shape[along:]) for a in arrays]
    both = jnp.concatenate(
        [a.reshape(*a.shape[:along], w) for a, w in zip(arrays, widths)], axis=along
    )
    out = lax.all_gather(both, axis, axis=dim, tiled=True)
    tiles = jnp.split(out, [sum(widths[:k]) for k in range(1, len(widths))], axis=along)
    return tuple((b.reshape(*out.shape[:along], *a.shape[along:]) for a, b in zip(arrays, tiles)))


def layer_norm(inputs):
    center = inputs - jnp.mean(inputs, axis=-1, keepdims=True)
    spread = jnp.mean(center * center, axis=-1, keepdims=True)
    return center * lax.rsqrt(spread + epsilon)


def attend(queries, key_part, value_part, keep_mask, bias_term):
    scores = jnp.einsum(
        "ihd,jhd->hij", queries, key_part, preferred_element_type=jnp.float32
    ) * HEAD_DEPTH ** (-0.5)
    if bias_term is not None:
        scores = scores + bias_term.astype(jnp.float32)
    scores = jnp.where(keep_mask[None, None, :] > 0, scores, -1000000000.0)
    weights = jax.nn.softmax(scores, axis=-1).astype(jnp.bfloat16)
    return jnp.einsum("hij,jhd->ihd", weights, value_part, preferred_element_type=jnp.float32)


def column_update(
    column, keep_column, column_proj, vertical_projector, expansion_matrix, contraction_matrix
):
    expanded_dimension = HEAD_TOTAL * HEAD_DEPTH
    standardized = layer_norm(column.astype(jnp.float32)).astype(jnp.bfloat16)
    projected = jnp.dot(standardized, column_proj, preferred_element_type=jnp.float32).astype(
        jnp.bfloat16
    )
    queries = projected[:, :expanded_dimension].reshape(-1, HEAD_TOTAL, HEAD_DEPTH)
    key_part = projected[:, expanded_dimension : 2 * expanded_dimension].reshape(
        -1, HEAD_TOTAL, HEAD_DEPTH
    )
    value_part = projected[:, 2 * expanded_dimension : 3 * expanded_dimension].reshape(
        -1, HEAD_TOTAL, HEAD_DEPTH
    )
    attended = attend(queries, key_part, value_part, keep_column, None).reshape(
        -1, expanded_dimension
    )
    sigmoid_scaled = (
        jax.nn.sigmoid(projected[:, 3 * expanded_dimension :].astype(jnp.float32)) * attended
    ).astype(jnp.bfloat16)
    mixed = column.astype(jnp.float32) + jnp.dot(
        sigmoid_scaled, vertical_projector, preferred_element_type=jnp.float32
    )
    inner = jnp.maximum(
        jnp.dot(
            layer_norm(mixed).astype(jnp.bfloat16),
            expansion_matrix,
            preferred_element_type=jnp.float32,
        ),
        0.0,
    ).astype(jnp.bfloat16)
    return (mixed + jnp.dot(inner, contraction_matrix, preferred_element_type=jnp.float32)).astype(
        jnp.bfloat16
    )


def body(
    homolog_tensor,
    pair_features,
    entry_real_mask,
    chain_ids,
    horizontal_matrices,
    horizontal_projector,
    bias_proj,
    chain_bias,
    column_proj,
    vertical_projector,
    expansion_matrix,
    contraction_matrix,
):
    row_count, local_residues, channels = homolog_tensor.shape
    expanded_dimension = HEAD_TOTAL * HEAD_DEPTH
    dap_count = lax.axis_size(DAP)
    pair_rows, pair_columns, pair_width = pair_features.shape
    normed_pair = layer_norm(pair_features.astype(jnp.float32))
    projected_pair = jnp.einsum(
        "ijc,ch->hij", normed_pair, bias_proj, precision=lax.Precision.HIGHEST
    )
    row_chain = lax.dynamic_slice_in_dim(chain_ids, lax.axis_index("seq") * pair_rows, pair_rows)
    column_chain = lax.dynamic_slice_in_dim(
        chain_ids, lax.axis_index(DAP) * pair_columns, pair_columns
    )
    same_chain = (row_chain[:, None] == column_chain[None, :]).astype(jnp.float32)
    chain_term = chain_bias[0][:, None, None] * same_chain + chain_bias[1][:, None, None] * (
        1.0 - same_chain
    )
    local_bias = (projected_pair + chain_term).astype(jnp.bfloat16)
    pair_bias = whole_of(local_bias, (("dap_0", "dap_1", "dap_2"), "dap_3"), 2)
    standardized = layer_norm(homolog_tensor.astype(jnp.float32)).astype(jnp.bfloat16)
    flat = standardized.reshape(-1, channels)
    keep_mask = entry_real_mask.astype(jnp.bfloat16)
    queries = (
        jnp.dot(
            flat, horizontal_matrices[:, :expanded_dimension], preferred_element_type=jnp.float32
        )
        .astype(jnp.bfloat16)
        .reshape(row_count, local_residues, expanded_dimension)
    )
    gating = (
        jnp.dot(
            flat,
            horizontal_matrices[:, 3 * expanded_dimension :],
            preferred_element_type=jnp.float32,
        )
        .astype(jnp.bfloat16)
        .reshape(row_count, local_residues, expanded_dimension)
    )
    normed_all, keep_all = side_by_side((standardized, keep_mask), "seq", 1, 2)
    key_values = (
        jnp.dot(
            normed_all.reshape(-1, channels),
            horizontal_matrices[:, expanded_dimension : 3 * expanded_dimension],
            preferred_element_type=jnp.float32,
        )
        .astype(jnp.bfloat16)
        .reshape(row_count, -1, 2 * expanded_dimension)
    )

    def one_row(inputs_row):
        row_queries, row_pairs, row_keep = inputs_row
        key_part = row_pairs[:, :expanded_dimension].reshape(-1, HEAD_TOTAL, HEAD_DEPTH)
        value_part = row_pairs[:, expanded_dimension:].reshape(-1, HEAD_TOTAL, HEAD_DEPTH)
        return attend(
            row_queries.reshape(local_residues, HEAD_TOTAL, HEAD_DEPTH),
            key_part,
            value_part,
            row_keep,
            pair_bias,
        ).reshape(local_residues, expanded_dimension)

    attended = lax.map(one_row, (queries, key_values, keep_all))
    sigmoid_scaled = (jax.nn.sigmoid(gating.astype(jnp.float32)) * attended).astype(jnp.bfloat16)
    row_result = jnp.dot(
        sigmoid_scaled.reshape(-1, expanded_dimension),
        horizontal_projector,
        preferred_element_type=jnp.float32,
    ).reshape(row_count, local_residues, channels)
    updated_rows = (homolog_tensor.astype(jnp.float32) + row_result).astype(jnp.bfloat16)
    per_device = local_residues // dap_count
    blocks = updated_rows.reshape(row_count, dap_count, per_device, channels)
    keep_blocks = keep_mask.reshape(row_count, dap_count, per_device)

    def single_column(inputs_col):
        return column_update(
            inputs_col[0],
            inputs_col[1],
            column_proj,
            vertical_projector,
            expansion_matrix,
            contraction_matrix,
        )

    column_block = lax.all_to_all(blocks, DAP, split_axis=1, concat_axis=0, tiled=True)
    column_keep = lax.all_to_all(keep_blocks, DAP, split_axis=1, concat_axis=0, tiled=True)
    inputs_col = (jnp.moveaxis(column_block[:, 0], 1, 0), jnp.moveaxis(column_keep[:, 0], 1, 0))
    output_list = lax.map(single_column, inputs_col)
    mixed = jnp.moveaxis(output_list, 0, 1)[:, None]
    returned = lax.all_to_all(mixed, DAP, split_axis=0, concat_axis=1, tiled=True)
    return returned.reshape(row_count, local_residues, channels)


def solution(mesh):
    torus = Mesh(
        mesh.devices.reshape(8, 2, 4, 2, mesh.shape["seq"]),
        ("dap_0", "dap_1", "dap_2", "dap_3", "seq"),
    )
    return jax.shard_map(
        body,
        mesh=torus,
        in_specs=(
            P(DAP, "seq", None),
            P("seq", DAP, None),
            P(DAP, "seq"),
            P(),
            P(),
            P(),
            P(),
            P(),
            P(),
            P(),
            P(),
            P(),
        ),
        out_specs=P(DAP, "seq", None),
        check_vma=False,
    )
```

profile of v0, /device:TPU:1, one launch (start us, length us, event | category | flops | bytes accessed | tf_op | source)
XLA Modules:
  0.0 114.0 jit_solution(2907823089189007500)
XLA Ops:
  0.0 0.8 dynamic_slice.21
  0.9 0.8 dynamic_slice.20
  1.8 1.1 convert_reduce_fusion
  2.9 1.3 %fusion.25 = f32[128,4]{1,0:T(8,128)S(1)} fusion(bf16[128,4,128]{2,1,0:T(4,128)(2,1)} %param.13, f32[128,4]{1,0:T(8,128)S(1)} %broadcast_multiply_fusion), kind=kLoop, calls=%fused_computation.41 | loop fusion | flops 261632 | bytes 135168 | tf_op jit(solution)/shard_map/reduce_sum | solution.py:46
  4.2 1.2 %fusion.23 = f32[128,4,128]{2,1,0:T(4,128)S(1)} fusion(bf16[128,4,128]{2,1,0:T(4,128)(2,1)} %param.13, f32[128,4]{1,0:T(8,128)S(1)} %add_rsqrt_fusion, f32[128,4]{1,0:T(8,128)S(1)} %broadcast_multiply_fusion), kind=kLoop, calls=%fused_computation.39 | loop fusion | flops 196608 | bytes 397312 | tf_op jit(solution)/shard_map/mul | solution.py:47
  5.5 0.8 slice_bitcast_fusion.3
  6.2 1.0 fusion.21
  7.2 0.9 broadcast_in_dim.77
  8.1 15.3 %all-to-all-start = ((bf16[64,8,128,4]{2,1,3,0:T(8,128)(2,1)}), bf16[64,8,128,4]{2,1,3,0:T(8,128)(2,1)S(1)}, u32[]{:S(2)}, u32[]{:S(2)}) async-start(bf16[64,8,128,4]{2,1,3,0:T(8,128)(2,1)} %broadcast_in_dim.77), calls=%async_computation | async-start | bytes 1048576 | tf_op jit(solution)/shard_map/all_to_all | solution.py:19
  23.6 0.8 copy.57
  25.2 15.5 %all_gather.3 = bf16[1,512,257]{2,1,0:T(8,128)(2,1)S(1)} all-gather(bf16[1,128,257]{2,1,0:T(8,128)(2,1)S(1)} %pad_maximum_fusion), channel_id=1, replica_groups=mesh['dap_0'=8,'dap_1'=2,'dap_2'=4,'dap_3'=2,'seq'=4] {'seq'}, dimensions={1}, use_global_device_ids=true | all-gather | bytes 328960 | tf_op jit(solution)/shard_map/all_gather | solution.py:39
  41.4 7.5 %all_to_all.37 = bf16[2,64,8,128,4]{3,2,4,1,0:T(8,128)(2,1)S(1)} all-to-all(bf16[2,64,8,128,4]{3,2,4,1,0:T(8,128)(2,1)S(1)} %broadcast_in_dim.78), channel_id=1, replica_groups=mesh['dap_0'=8,'dap_1'=2,'dap_2'=4,'dap_3'=2,'seq'=4] {'dap_3'}, dimensions={0} | all-to-all | bytes 2097152 | tf_op jit(solution)/shard_map/all_to_all | solution.py:19
  48.9 11.3 %all-to-all-start.3 = ((bf16[1,128,1]{2,0,1:T(2,128)(2,1)}), bf16[1,128,1]{2,0,1:T(2,128)(2,1)S(1)}, u32[]{:S(2)}, u32[]{:S(2)}) async-start(bf16[1,128,1]{2,0,1:T(2,128)(2,1)} %copy.57), calls=%async_computation.3 | async-start | bytes 131072 | tf_op jit(solution)/shard_map/all_to_all | solution.py:195
  60.7 1.9 %copy.52 = f32[8,128,512]{2,1,0:T(8,128)} copy(f32[8,128,512]{1,0,2:T(8,128)S(1)} %bitcast.93) | data formatting | bytes 4194304 | tf_op jit(solution)/shard_map/while/body/eval_jaxpr/convert_element_type | solution.py:55
  62.6 2.1 %add_select_fusion = f32[8,128,512]{2,1,0:T(8,128)S(1)} fusion(f32[8,128,512]{2,1,0:T(8,128)} %copy.52, bf16[128,8,32]{0,2,1:T(8,128)(2,1)S(1)} %bitcast.97, bf16[512,8,32]{0,2,1:T(8,128)(2,1)S(1)} %bitcast.94, pred[512]{0:T(512)(128)(4,1)S(1)} %compare_reduce_fusion.1), kind=kOutput, calls=%fused_computation.5 | convolution fusion | flops 35127296 | bytes 4522496 | tf_op jit(solution)/shard_map/while/body/eval_jaxpr/ihd,jhd->hij/dot_general | solution.py:51
  65.3 1.9 %fusion.22 = f32[8,32,128]{2,1,0:T(8,128)S(1)} fusion(bf16[512,8,32]{0,2,1:T(8,128)(2,1)S(1)} %bitcast.102, f32[8,128]{1,0:T(8,128)S(1)} %fusion.68, f32[8,128,512]{2,1,0:T(8,128)S(1)} %add_select_fusion), kind=kOutput, calls=%fused_computation.35 | convolution fusion | flops 35128832 | bytes 2494464 | tf_op jit(solution)/shard_map/while/body/eval_jaxpr/hij,jhd->ihd/dot_general | solution.py:58
  67.3 1.3 %fusion.18 = bf16[1,128,1,256]{3,1,2,0:T(8,128)(2,1)S(1)} fusion(bf16[256,256]{1,0:T(8,128)(2,1)S(1)} %copy-done.5, f32[128,256]{1,0:T(8,128)S(1)} %copy.53, bf16[1,128,256]{2,1,0:T(8,128)(2,1)S(1)} %copy-done.1, bf16[256,1024]{1,0:T(8,128)(2,1)} %param.16, f32[128]{0:T(128)S(1)} %add_rsqrt_fusion.3, f32[128]{0:T(128)S(1)} %broadcast_multiply_fusion.3), kind=kOutput, calls=%fused_computation.30 | convolution fusion | flops 34013184 | bytes 590848 | tf_op jit(solution)/shard_map/dot_general | solution.py:174
  69.3 1.1 reduce.7
  70.4 0.7 reshape.245
  71.0 12.3 %all-to-all-start.2 = ((bf16[128,2,128]{2,1,0:T(2,128)(2,1)}), bf16[128,2,128]{2,1,0:T(2,128)(2,1)S(1)}, u32[]{:S(2)}, u32[]{:S(2)}) async-start(bf16[128,2,128]{2,1,0:T(2,128)(2,1)} %reshape.245), calls=%async_computation.2 | async-start | bytes 131072 | tf_op jit(solution)/shard_map/all_to_all | solution.py:194
  83.3 2.4 %compare_reduce_fusion = pred[128]{0:T(512)(128)(4,1)S(1)} fusion(bf16[1,128,1]{2,0,1:T(2,128)(2,1)S(1)} %all-to-all-done.3), kind=kLoop, calls=%fused_computation.47 | loop fusion | flops 128 | bytes 384 | tf_op jit(solution)/shard_map/while/body/eval_jaxpr/gt | solution.py:56
  85.7 8.1 %all-to-all-done.2 = bf16[128,2,128]{2,1,0:T(2,128)(2,1)S(1)} async-done(((bf16[128,2,128]{2,1,0:T(2,128)(2,1)}), bf16[128,2,128]{2,1,0:T(2,128)(2,1)S(1)}, u32[]{:S(2)}, u32[]{:S(2)}) %all-to-all-start.2) | async-done | bytes 65568 | tf_op jit(solution)/shard_map/all_to_all | solution.py:194
  96.8 0.7 reduce.8
  97.5 15.8 %all_to_all.38 = bf16[128,2,128]{2,1,0:T(2,128)(2,1)S(1)} all-to-all(bf16[128,2,128]{2,1,0:T(2,128)(2,1)S(1)} %reshape.247), channel_id=1, replica_groups=mesh['dap_0'=8,'dap_1'=2,'dap_2'=4,'dap_3'=2,'seq'=4] {'dap_0','dap_1','..., dimensions={0} | all-to-all | bytes 131072 | tf_op jit(solution)/shard_map/all_to_all | solution.py:199
  (64 shorter events, 7.2 us)
Async XLA Ops:
  0.0 94.1 %copy-start = (bf16[256,1024]{1,0:T(8,128)(2,1)S(1)}, bf16[256,1024]{1,0:T(8,128)(2,1)}, u32[]{:S(2)}) copy-start(bf16[256,1024]{1,0:T(8,128)(2,1)} %param.20) | copy-start | bytes 1572868
  0.0 23.5 %copy-start.7 = (s32[1,128]{1,0:T(1,128)S(1)}, s32[1,128]{1,0:T(1,128)}, u32[]{:S(2)}) copy-start(s32[1,128]{1,0:T(1,128)} %param.14) | copy-start | bytes 1540
  0.0 24.4 %copy-start.1 = (bf16[1,128,256]{2,1,0:T(8,128)(2,1)S(1)}, bf16[1,128,256]{2,1,0:T(8,128)(2,1)}, u32[]{:S(2)}) copy-start(bf16[1,128,256]{2,1,0:T(8,128)(2,1)} %param.12) | copy-start | bytes 196612
  0.0 24.7 %copy-start.4 = (bf16[256,1024]{1,0:T(8,128)(2,1)S(1)}, bf16[256,1024]{1,0:T(8,128)(2,1)}, u32[]{:S(2)}) copy-start(bf16[256,1024]{1,0:T(8,128)(2,1)} %param.16) | copy-start | bytes 1572868
  8.1 33.1 %all-to-all-start = ((bf16[64,8,128,4]{2,1,3,0:T(8,128)(2,1)}), bf16[64,8,128,4]{2,1,3,0:T(8,128)(2,1)S(1)}, u32[]{:S(2)}, u32[]{:S(2)}) async-start(bf16[64,8,128,4]{2,1,3,0:T(8,128)(2,1)} %broadcast_in_dim.77), calls=%async_computation | async-start | bytes 1048576 | tf_op jit(solution)/shard_map/all_to_all | solution.py:19
  48.9 22.2 %all-to-all-start.3 = ((bf16[1,128,1]{2,0,1:T(2,128)(2,1)}), bf16[1,128,1]{2,0,1:T(2,128)(2,1)S(1)}, u32[]{:S(2)}, u32[]{:S(2)}) async-start(bf16[1,128,1]{2,0,1:T(2,128)(2,1)} %copy.57), calls=%async_computation.3 | async-start | bytes 131072 | tf_op jit(solution)/shard_map/all_to_all | solution.py:195
  65.3 2.1 %copy-start.5 = (bf16[256,256]{1,0:T(8,128)(2,1)S(1)}, bf16[256,256]{1,0:T(8,128)(2,1)}, u32[]{:S(2)}) copy-start(bf16[256,256]{1,0:T(8,128)(2,1)} %param.17) | copy-start | bytes 393220
  71.0 22.7 %all-to-all-start.2 = ((bf16[128,2,128]{2,1,0:T(2,128)(2,1)}), bf16[128,2,128]{2,1,0:T(2,128)(2,1)S(1)}, u32[]{:S(2)}, u32[]{:S(2)}) async-start(bf16[128,2,128]{2,1,0:T(2,128)(2,1)} %reshape.245), calls=%async_computation.2 | async-start | bytes 131072 | tf_op jit(solution)/shard_map/all_to_all | solution.py:194
  94.7 1.2 %copy-start.6 = (bf16[256,256]{1,0:T(8,128)(2,1)S(1)}, bf16[256,256]{1,0:T(8,128)(2,1)}, u32[]{:S(2)}) copy-start(bf16[256,256]{1,0:T(8,128)(2,1)} %param.21) | copy-start | bytes 393220
  95.0 1.4 %copy-start.2 = (bf16[1024,256]{1,0:T(8,128)(2,1)S(1)}, bf16[1024,256]{1,0:T(8,128)(2,1)}, u32[]{:S(2)}) copy-start(bf16[1024,256]{1,0:T(8,128)(2,1)} %param.23) | copy-start | bytes 1572868
  95.0 1.3 %copy-start.3 = (bf16[256,1024]{1,0:T(8,128)(2,1)S(1)}, bf16[256,1024]{1,0:T(8,128)(2,1)}, u32[]{:S(2)}) copy-start(bf16[256,1024]{1,0:T(8,128)(2,1)} %param.22) | copy-start | bytes 1572868
where the time goes:
time: 115 us; the launch traced here: 114 us
  starting transfers between devices  38.9 us (34%)
  blocking collectives  38.8 us (34%)
  other arithmetic  9.8 us (9%)
  local copies, waits for them, and re-layouts  9.24 us (8%)
  matrix products  8.72 us (8%)
  waiting for transfers between devices  8.12 us (7%)
    all_to_all x1, blocking collectives, body(): lax.all_to_all(mixed, DAP, split_axis=0, concat_axis=1, tiled=True)  15.8 us
    all_gather x1, blocking collectives, side_by_side(): out = lax.all_gather(both, axis, axis=dim, tiled=True)  15.5 us
    all_to_all x1, starting transfers between devices, sent_to_all(): return lax.all_to_all(copies, axis, split_axis=0, concat_axis=0, tiled=True)  15.3 us
    all_to_all x1, starting transfers between devices, body(): lax.all_to_all(blocks, DAP, split_axis=1, concat_axis=0, tiled=True)  12.3 us
    all_to_all x1, starting transfers between devices, body(): lax.all_to_all(keep_blocks, DAP, split_axis=1, concat_axis=0, tiled=True)  11.3 us
    all_to_all x1, waiting for transfers between devices, body(): lax.all_to_all(blocks, DAP, split_axis=1, concat_axis=0, tiled=True)  8.11 us
    all_to_all x1, blocking collectives, sent_to_all(): return lax.all_to_all(copies, axis, split_axis=0, concat_axis=0, tiled=True)  7.49 us
    gt x2, other arithmetic, attend(): scores = jnp.where(keep_mask[None, None, :] > 0, scores, -1000000000.0)  2.51 us
  transfers between devices with their start and end apart: 3, of which 1 were waited for; matrix products, arithmetic and copies ran while one was open for 13% of the time, Pallas kernels for 0%

commit v1 on v0

v1 whole, which is shorter than its diff:
```python
import jax
import jax.numpy as jnp
from jax import lax
from jax.experimental import pallas as pl
from jax.experimental.pallas import tpu as pltpu
from jax.sharding import Mesh
from jax.sharding import PartitionSpec as P

HEADS = 8
DEPTH = 32
WIDE = 256
SCALE = DEPTH ** (-0.5)
EPS = 1e-05
DAP = ("dap_0", "dap_1", "dap_2", "dap_3")
MESH = pl.DeviceIdType.MESH
F32 = jnp.float32
BF16 = jnp.bfloat16


def layer_norm(x):
    center = x - jnp.mean(x, axis=-1, keepdims=True)
    spread = jnp.mean(center * center, axis=-1, keepdims=True)
    return center * lax.rsqrt(spread + EPS)


def mm(a, b):
    return jnp.dot(a, b, preferred_element_type=F32)


def plane_id(k):
    return {"dap_1": lax.div(k, 8), "dap_2": lax.rem(lax.div(k, 2), 4), "dap_3": lax.rem(k, 2)}


def kernel(
    hom, pair, mask, chain_v, bproj, chain_s, cbias, wh_h, ph_h, wc_h, pv_h, ex_h, co_h,
    out,
    wh, ph, wc, pv, ex, co,
    xs, plane, biasall, homall, mrow, mcol, keep, keepc,
    qbd, vt, scores, ot, gt,
    a1, a2s, a2, b1s, b1, b2s, b2, fs,
    wsem, plane_s, plane_r, hom_s, hom_r, mrow_s, mrow_r, mp_s, mp_r, mz_s, mz_r,
    ring_s, ring_r, part_s, part_r, a1_s, a1_r, a2_ss, a2_r, b1_ss, b1_r, b2_ss, b2_r,
):
    z = lax.axis_index("dap_0")
    y = lax.axis_index("dap_1")
    x = lax.axis_index("dap_2")
    c = lax.axis_index("dap_3")
    seq = lax.axis_index("seq")
    k = y * 8 + x * 2 + c
    dap = z * 16 + k

    loads = [pltpu.make_async_copy(s, d, wsem.at[n]) for n, (s, d) in enumerate(
        ((wh_h, wh), (ph_h, ph), (wc_h, wc), (pv_h, pv), (ex_h, ex), (co_h, co)))]
    for ld in loads:
        ld.start()

    def remote(src, dst, ss, rs, device):
        return pltpu.make_async_remote_copy(
            src_ref=src, dst_ref=dst, send_sem=ss, recv_sem=rs, device_id=device,
            device_id_type=MESH)

    barrier = pltpu.get_barrier_semaphore()

    @pl.loop(1, 16)
    def _(p):
        pl.semaphore_signal(barrier, inc=1, device_id=plane_id(lax.rem(k + p, 16)), device_id_type=MESH)

    @pl.loop(1, 8)
    def _(p):
        pl.semaphore_signal(barrier, inc=1, device_id={"dap_0": lax.rem(z + p, 8)}, device_id_type=MESH)

    @pl.loop(1, 4)
    def _(p):
        pl.semaphore_signal(barrier, inc=1, device_id={"seq": lax.rem(seq + p, 4)}, device_id_type=MESH)

    xs[...] = layer_norm(pair[...].astype(F32))
    bt = bproj[...].T
    head = lax.broadcasted_iota(jnp.int32, (8, 128), 0)
    cb0 = jnp.zeros((8, 128), F32)
    cb1 = jnp.zeros((8, 128), F32)
    for h in range(HEADS):
        cb0 = jnp.where(head == h, cbias[h], cb0)
        cb1 = jnp.where(head == h, cbias[HEADS + h], cb1)
    row_chain = jnp.broadcast_to(chain_v[pl.ds(seq, 1), :], (8, 128))
    parts = []
    for j in range(4):
        xj = xs[pl.ds(j, 128, stride=4), :]
        pj = lax.dot_general(bt, xj, (((1,), (1,)), ((), ())), precision=lax.Precision.HIGHEST,
                             preferred_element_type=F32)
        parts.append(pj + jnp.where(row_chain == chain_s[dap * 4 + j], cb0, cb1))
    plane[k] = jnp.concatenate(parts, axis=0).astype(BF16)
    homall[seq] = hom[...]
    mrow[seq] = mask[...]
    mcol[z, k] = mask[...]
    qbd[...] = jnp.zeros_like(qbd)

    pl.semaphore_wait(barrier, 25)

    def plane_copy(p):
        to = lax.rem(k + p, 16)
        return remote(plane.at[k], plane.at[k], plane_s.at[to], plane_r.at[k], plane_id(to))

    def plane_recv(p):
        fr = lax.rem(k + p, 16)
        return remote(plane.at[fr], plane.at[fr], plane_s.at[fr], plane_r.at[fr], plane_id(fr))

    def hom_copy(p):
        to = lax.rem(seq + p, 4)
        return remote(hom, homall.at[seq], hom_s.at[to], hom_r.at[seq], {"seq": to})

    def hom_recv(p):
        fr = lax.rem(seq + p, 4)
        return remote(hom, homall.at[fr], hom_s.at[fr], hom_r.at[fr], {"seq": fr})

    def mrow_copy(p):
        to = lax.rem(seq + p, 4)
        return remote(mask, mrow.at[seq], mrow_s.at[to], mrow_r.at[seq], {"seq": to})

    def mrow_recv(p):
        fr = lax.rem(seq + p, 4)
        return remote(mask, mrow.at[fr], mrow_s.at[fr], mrow_r.at[fr], {"seq": fr})

    def mp_copy(p):
        to = lax.rem(k + p, 16)
        return remote(mask, mcol.at[z, k], mp_s.at[to], mp_r.at[k], plane_id(to))

    def mp_recv(p):
        fr = lax.rem(k + p, 16)
        return remote(mask, mcol.at[z, fr], mp_s.at[fr], mp_r.at[fr], plane_id(fr))

    def mz_copy(p):
        to = lax.rem(z + p, 8)
        return remote(mcol.at[z], mcol.at[z], mz_s.at[to], mz_r.at[z], {"dap_0": to})

    def mz_recv(p):
        fr = lax.rem(z + p, 8)
        return remote(mcol.at[fr], mcol.at[fr], mz_s.at[fr], mz_r.at[fr], {"dap_0": fr})

    pl.loop(1, 16)(lambda p: plane_copy(p).start())
    pl.loop(1, 4)(lambda p: mrow_copy(p).start())
    pl.loop(1, 4)(lambda p: hom_copy(p).start())
    pl.loop(1, 16)(lambda p: mp_copy(p).start())

    def transposed(v):
        return v.astype(BF16).T

    def spread_queries(qt):
        for h in range(HEADS):
            qbd[h * 32:(h + 1) * 32, h * 128:(h + 1) * 128] = qt[h * 32:(h + 1) * 32, :]

    def block_scores(b, keys, values):
        scores[pl.ds(pl.multiple_of(b * 128, 128), 128), :] = mm(keys.astype(BF16), qbd[...])
        vt[:, pl.ds(pl.multiple_of(b * 128, 128), 128)] = transposed(values)

    loads[0].wait()
    own = hom[...].astype(F32)
    qkvg = mm(layer_norm(own).astype(BF16), wh[...])
    spread_queries(transposed(qkvg[:, :WIDE]))
    gt[...] = transposed(qkvg[:, 3 * WIDE:]).astype(F32)
    block_scores(seq, qkvg[:, WIDE:2 * WIDE], qkvg[:, 2 * WIDE:3 * WIDE])

    def neighbour_block(p):
        b = lax.rem(seq + p, 4)
        hom_recv(p).wait_recv()
        kv = mm(layer_norm(homall[b].astype(F32)).astype(BF16), wh[:, WIDE:3 * WIDE])
        block_scores(b, kv[:, :WIDE], kv[:, WIDE:])

    pl.loop(1, 16)(lambda p: plane_recv(p).wait_recv())
    xs[...] = plane[...].reshape(512, 128).astype(F32)
    for h in range(HEADS):
        biasall[z, :, h * 128:(h + 1) * 128] = xs[pl.ds(h, 64, stride=8), :].astype(BF16)

    step = 1 - 2 * c
    onward = {"dap_0": lax.rem(z + step + 8, 8)}
    partner = {"dap_3": 1 - c}

    def piece(block, q):
        return biasall.at[block, pl.ds(pl.multiple_of(q * 32, 32), 32)]

    def ring_copy(s, i):
        b = lax.rem(z - step * s + 8, 8)
        ref = piece(b, lax.rem(c + i, 2))
        return remote(ref, ref, ring_s.at[s, i], ring_r.at[s, i], onward)

    def ring_recv(s, i):
        b = lax.rem(z - step * (s + 1) + 8, 8)
        ref = piece(b, lax.rem(c + i, 2))
        return remote(ref, ref, ring_s.at[s, i], ring_r.at[s, i], onward)

    def part_copy(s, i):
        b = lax.rem(z - step * (s + 1) + 8, 8)
        ref = piece(b, lax.rem(c + i, 2))
        return remote(ref, ref, part_s.at[s, i], part_r.at[s, i], partner)

    def part_recv(s, i):
        b = lax.rem(z + step * (s + 1) + 8, 8)
        ref = piece(b, lax.rem(1 - c + i, 2))
        return remote(ref, ref, part_s.at[s, i], part_r.at[s, i], partner)

    hops = [(s, i) for s in range(4) for i in range(2) if s < 3 or i == 0]
    for i in range(2):
        ring_copy(0, i).start()
    pl.loop(1, 16)(lambda p: mp_recv(p).wait_recv())
    pl.loop(1, 8)(lambda p: mz_copy(p).start())
    for s, i in hops:
        ring_recv(s, i).wait_recv()
        if (s + 1, i) in hops:
            ring_copy(s + 1, i).start()
        part_copy(s, i).start()
        if (s, i) == (0, 1):
            neighbour_block(1)
            neighbour_block(3)
        if (s, i) == (1, 1):
            neighbour_block(2)
            pl.loop(1, 4)(lambda p: mrow_recv(p).wait_recv())
            for b in range(4):
                keep[b * 128:(b + 1) * 128, :] = jnp.broadcast_to(mrow[b].astype(F32), (128, 128)).T
        if (s, i) == (2, 0):
            pl.loop(1, 8)(lambda p: mz_recv(p).wait_recv())
            fs[:128, :] = mcol[...].reshape(128, 128).astype(F32)
            pick = (lax.broadcasted_iota(jnp.int32, (128, 128), 0) == dap).astype(BF16)
            rows = [fs[pl.ds(n, 8, stride=16), :] for n in range(16)]
            keepc[...] = mm(jnp.concatenate(rows, axis=0).astype(BF16), pick)
    for s, i in hops:
        part_recv(s, i).wait_recv()

    def softmax_out(s, vth):
        m = jnp.max(s, axis=0, keepdims=True)
        e = jnp.exp(s - m)
        w = (e * (1.0 / jnp.sum(e, axis=0, keepdims=True))).astype(BF16)
        return mm(vth, w)

    for h in range(HEADS):
        lanes = slice(h * 128, (h + 1) * 128)
        s = scores[:, lanes] * SCALE + biasall[:, :, lanes].reshape(512, 128).astype(F32)
        s = jnp.where(keep[...] > 0.0, s, -1000000000.0)
        ot[h * 32:(h + 1) * 32, :] = softmax_out(s, vt[h * 32:(h + 1) * 32, :])

    def split(v):
        fs[:128, :] = v[:, :128].astype(F32)
        fs[128:, :] = v[:, 128:].astype(F32)

    def gated_project(w):
        g = (jax.nn.sigmoid(gt[...]) * ot[...]).astype(BF16)
        return mm(g.T, w)

    loads[1].wait()
    one = (hom[...].astype(F32) + gated_project(ph[...])).astype(BF16)
    b2s[...] = one.reshape(8, 16, WIDE)
    a1[z] = b2s[z]

    def a1_copy(p):
        to = lax.rem(z + p, 8)
        return remote(b2s.at[to], a1.at[z], a1_s.at[to], a1_r.at[z], {"dap_0": to})

    def a1_recv(p):
        fr = lax.rem(z + p, 8)
        return remote(b2s.at[fr], a1.at[fr], a1_s.at[fr], a1_r.at[fr], {"dap_0": fr})

    pl.loop(1, 8)(lambda p: a1_copy(p).start())
    pl.loop(1, 8)(lambda p: a1_recv(p).wait_recv())

    split(a1[...].reshape(128, WIDE))
    for n in range(16):
        for t in range(2):
            a2s[n, :, t * 128:(t + 1) * 128] = fs[pl.ds(t * 128 + n, 8, stride=16), :].astype(BF16)
    a2[k] = a2s[k]

    def a2_copy(p):
        to = lax.rem(k + p, 16)
        return remote(a2s.at[to], a2.at[k], a2_ss.at[to], a2_r.at[k], plane_id(to))

    def a2_recv(p):
        fr = lax.rem(k + p, 16)
        return remote(a2s.at[fr], a2.at[fr], a2_ss.at[fr], a2_r.at[fr], plane_id(fr))

    pl.loop(1, 16)(lambda p: a2_copy(p).start())
    loads[2].wait()
    loads[3].wait()
    loads[4].wait()
    loads[5].wait()
    pl.loop(1, 16)(lambda p: a2_recv(p).wait_recv())

    col = a2[...].astype(F32).reshape(128, WIDE)
    qkvg = mm(layer_norm(col).astype(BF16), wc[...])
    spread_queries(transposed(qkvg[:, :WIDE]))
    gt[...] = transposed(qkvg[:, 3 * WIDE:]).astype(F32)
    cs = mm(qkvg[:, WIDE:2 * WIDE].astype(BF16), qbd[...]) * SCALE
    cvt = transposed(qkvg[:, 2 * WIDE:3 * WIDE])
    for h in range(HEADS):
        s = jnp.where(keepc[...] > 0.0, cs[:, h * 128:(h + 1) * 128], -1000000000.0)
        ot[h * 32:(h + 1) * 32, :] = softmax_out(s, cvt[h * 32:(h + 1) * 32, :])
    two = col + gated_project(pv[...])
    inner = jnp.maximum(mm(layer_norm(two).astype(BF16), ex[...]), 0.0).astype(BF16)
    done = two + mm(inner, co[...])
    b1s[...] = done.reshape(16, 8, WIDE).astype(BF16)
    b1[k] = b1s[k]

    def b1_copy(p):
        to = lax.rem(k + p, 16)
        return remote(b1s.at[to], b1.at[k], b1_ss.at[to], b1_r.at[k], plane_id(to))

    def b1_recv(p):
        fr = lax.rem(k + p, 16)
        return remote(b1s.at[fr], b1.at[fr], b1_ss.at[fr], b1_r.at[fr], plane_id(fr))

    pl.loop(1, 16)(lambda p: b1_copy(p).start())
    pl.loop(1, 8)(lambda p: a1_copy(p).wait_send())
    pl.loop(1, 16)(lambda p: b1_recv(p).wait_recv())
    split(b1[...].astype(F32).reshape(128, WIDE))
    for n in range(8):
        for t in range(2):
            b2s[n, :, t * 128:(t + 1) * 128] = fs[pl.ds(t * 128 + n, 16, stride=8), :].astype(BF16)
    b2[z] = b2s[z]

    def b2_copy(p):
        to = lax.rem(z + p, 8)
        return remote(b2s.at[to], b2.at[z], b2_ss.at[to], b2_r.at[z], {"dap_0": to})

    def b2_recv(p):
        fr = lax.rem(z + p, 8)
        return remote(b2s.at[fr], b2.at[fr], b2_ss.at[fr], b2_r.at[fr], {"dap_0": fr})

    pl.loop(1, 8)(lambda p: b2_copy(p).start())

    pl.loop(1, 16)(lambda p: plane_copy(p).wait_send())
    pl.loop(1, 16)(lambda p: mp_copy(p).wait_send())
    pl.loop(1, 16)(lambda p: a2_copy(p).wait_send())
    pl.loop(1, 16)(lambda p: b1_copy(p).wait_send())
    pl.loop(1, 8)(lambda p: mz_copy(p).wait_send())
    pl.loop(1, 4)(lambda p: hom_copy(p).wait_send())
    pl.loop(1, 4)(lambda p: mrow_copy(p).wait_send())
    for s, i in hops:
        ring_copy(s, i).wait_send()
        part_copy(s, i).wait_send()

    pl.loop(1, 8)(lambda p: b2_recv(p).wait_recv())
    pl.loop(1, 8)(lambda p: b2_copy(p).wait_send())
    out[...] = b2[...].reshape(128, WIDE)


def body(
    homolog_tensor, pair_features, entry_real_mask, chain_ids, horizontal_matrices,
    horizontal_projector, bias_proj, chain_bias, column_proj, vertical_projector,
    expansion_matrix, contraction_matrix,
):
    vmem = pl.BlockSpec(memory_space=pltpu.VMEM)
    smem = pl.BlockSpec(memory_space=pltpu.SMEM)
    hbm = pl.BlockSpec(memory_space=pl.ANY)
    dma = pltpu.SemaphoreType.DMA
    updated = pl.pallas_call(
        kernel,
        name="msa_block",
        out_shape=jax.ShapeDtypeStruct((128, WIDE), BF16),
        in_specs=[vmem] * 5 + [smem] * 2 + [hbm] * 6,
        out_specs=vmem,
        scratch_shapes=[
            pltpu.VMEM((WIDE, 4 * WIDE), BF16),
            pltpu.VMEM((WIDE, WIDE), BF16),
            pltpu.VMEM((WIDE, 4 * WIDE), BF16),
            pltpu.VMEM((WIDE, WIDE), BF16),
            pltpu.VMEM((WIDE, 4 * WIDE), BF16),
            pltpu.VMEM((4 * WIDE, WIDE), BF16),
            pltpu.VMEM((512, 128), F32),
            pltpu.VMEM((16, 32, 128), BF16),
            pltpu.VMEM((8, 64, 1024), BF16),
            pltpu.VMEM((4, 128, WIDE), BF16),
            pltpu.VMEM((4, 1, 128), jnp.int32),
            pltpu.VMEM((8, 16, 1, 128), jnp.int32),
            pltpu.VMEM((512, 128), F32),
            pltpu.VMEM((128, 128), F32),
            pltpu.VMEM((WIDE, 1024), BF16),
            pltpu.VMEM((WIDE, 512), BF16),
            pltpu.VMEM((512, 1024), F32),
            pltpu.VMEM((WIDE, 128), F32),
            pltpu.VMEM((WIDE, 128), F32),
            pltpu.VMEM((8, 16, WIDE), BF16),
            pltpu.VMEM((16, 8, WIDE), BF16),
            pltpu.VMEM((16, 8, WIDE), BF16),
            pltpu.VMEM((16, 8, WIDE), BF16),
            pltpu.VMEM((16, 8, WIDE), BF16),
            pltpu.VMEM((8, 16, WIDE), BF16),
            pltpu.VMEM((8, 16, WIDE), BF16),
            pltpu.VMEM((256, 128), F32),
            dma((6,)), dma((16,)), dma((16,)), dma((4,)), dma((4,)), dma((4,)), dma((4,)),
            dma((16,)), dma((16,)), dma((8,)), dma((8,)),
            dma((4, 2)), dma((4, 2)), dma((4, 2)), dma((4, 2)),
            dma((8,)), dma((8,)), dma((16,)), dma((16,)), dma((16,)), dma((16,)), dma((8,)), dma((8,)),
        ],
        compiler_params=pltpu.CompilerParams(collective_id=0, has_side_effects=True),
    )(
        homolog_tensor.reshape(128, WIDE),
        pair_features.reshape(512, 128),
        entry_real_mask,
        chain_ids.reshape(4, 128),
        bias_proj,
        chain_ids,
        chain_bias.reshape(16),
        horizontal_matrices,
        horizontal_projector,
        column_proj,
        vertical_projector,
        expansion_matrix,
        contraction_matrix,
    )
    return updated.reshape(1, 128, WIDE)


def solution(mesh):
    torus = Mesh(
        mesh.devices.reshape(8, 2, 4, 2, mesh.shape["seq"]),
        ("dap_0", "dap_1", "dap_2", "dap_3", "seq"),
    )
    return jax.shard_map(
        body,
        mesh=torus,
        in_specs=(P(DAP, "seq", None), P("seq", DAP, None), P(DAP, "seq")) + (P(),) * 9,
        out_specs=P(DAP, "seq", None),
        check_vma=False,
    )
```

time: 115 us -> 65 us (0.57)
  Pallas kernels: 0 us -> 61.3 us
  starting transfers between devices: 38.9 us -> 0 us
  blocking collectives: 38.8 us -> 0 us
  other arithmetic: 9.8 us -> 0 us
  matrix products: 8.72 us -> 0 us
  waiting for transfers between devices: 8.12 us -> 0 us
  local copies, waits for them, and re-layouts: 9.24 us -> 3.48 us
    pallas_call x0 -> x1, Pallas kernels: none -> 61.3 us  [body(): pl.pallas_call(kernel, name='msa_block', out_shape=jax.ShapeDtypeStruct((...]
    all_to_all x3 -> x0, starting transfers between devices: 38.9 us -> none  [the longest x1 15.3 us: sent_to_all(): return lax.all_to_all(copies, axis, split_axis=0, concat_axis=0, tiled=True)]
    all_to_all x2 -> x0, blocking collectives: 23.3 us -> none  [the longest x1 15.8 us: body(): lax.all_to_all(mixed, DAP, split_axis=0, concat_axis=1, tiled=True)]
    all_gather x1 -> x0, blocking collectives: 15.5 us -> none  [side_by_side(): out = lax.all_gather(both, axis, axis=dim, tiled=True)]
    dot_general x11 -> x0, matrix products: 8.35 us -> none  [the longest x2 2.37 us: attend(): jnp.einsum('ihd,jhd->hij', queries, key_part, preferred_element_type=jnp....]
    all_to_all x3 -> x0, waiting for transfers between devices: 8.12 us -> none  [the longest x1 8.11 us: body(): lax.all_to_all(blocks, DAP, split_axis=1, concat_axis=0, tiled=True)]
    reduce_sum x7 -> x0, other arithmetic: 3.12 us -> none  [the longest x4 1.8 us: layer_norm(): spread = jnp.mean(center * center, axis=-1, keepdims=True)]
    gt x2 -> x0, other arithmetic: 2.51 us -> none  [attend(): scores = jnp.where(keep_mask[None, None, :] > 0, scores, -1000000000.0)]
  transfers between devices with their start and end apart: 3 -> 0, of which waited for: 1 -> 0; matrix products, arithmetic and copies ran while one was open for 13% -> 0% of each run, Pallas kernels for 0% -> 0%
where the time goes in v1:
time: 65 us; the launch traced here: 64.8 us
  Pallas kernels  61.3 us (94%)
  local copies, waits for them, and re-layouts  3.48 us (5%)
    pallas_call x1, Pallas kernels, body(): pl.pallas_call(kernel, name='msa_block', out_shape=jax.ShapeDtypeStruct((...  61.3 us
    unnamed x6, local copies, waits for them, and re-layouts  2.9 us

profile of v1, /device:TPU:1, one launch (start us, length us, event | category | flops | bytes accessed | tf_op | source)
XLA Modules:
  0.0 64.8 jit_solution(244757105086127901)
XLA Ops:
  0.0 0.0 copy-start
  0.0 0.0 copy-start.1
  0.0 0.7 %copy-done.1 = f32[2,8]{1,0:T(2,128)S(1)} copy-done((f32[2,8]{1,0:T(2,128)S(1)}, f32[2,8]{1,0:T(2,128)}, u32[]{:S(2)}) %copy-start.1) | copy-done | bytes 88
  0.7 0.6 reshape.18.cbias
  1.3 0.0 copy-done
  1.3 0.7 %copy.13.bproj = f32[128,8]{1,0:T(8,128)} copy(f32[128,8]{0,1:T(8,128)S(1)} %copy-done) | data formatting | bytes 8192 | tf_op args[6]
  2.0 61.3 %msa_block.1 = bf16[128,256]{1,0:T(8,128)(2,1)} custom-call(bf16[128,256]{1,0:T(8,128)(2,1)} %bitcast.6, bf16[512,128]{1,0:T(8,128)(2,1)} %bitcast.5, s32[1,128]{1,0:T(1,128)} %mask.1, s32[4,128]{1,0:T(4,128)} %bitcast.7, f32[128,8]{1,0:T(8,128)} %copy.13.bproj, s32[512]{0:T(512)} %chain_s.1, f32[16]{0:T(128)} %reshape.18.cbias, bf16[256,1024]{1,0:T(8,128)(2,1)} %wh_h.1, ...), custom_call_target="tpu_custom_call" | custom-call | tf_op jit(solution)/shard_map/msa_block/pallas_call | solution.py:351
  63.3 1.5 %copy.15 = bf16[1,128,256]{2,1,0:T(8,128)(2,1)} copy(bf16[1,128,256]{2,1,0:T(8,128)(2,1)} %bitcast.4) | data formatting | bytes 131072
Async XLA Ops:
  0.0 1.3 %copy-start = (f32[128,8]{0,1:T(8,128)S(1)}, f32[128,8]{0,1:T(8,128)}, u32[]{:S(2)}) copy-start(f32[128,8]{0,1:T(8,128)} %param.18) | copy-start | bytes 12292
  0.0 0.7 %copy-start.1 = (f32[2,8]{1,0:T(2,128)S(1)}, f32[2,8]{1,0:T(2,128)}, u32[]{:S(2)}) copy-start(f32[2,8]{1,0:T(2,128)} %param.19) | copy-start | bytes 196

commit v2 on v1

v2 whole, which is shorter than its diff:
```python
import jax
import jax.numpy as jnp
from jax import lax
from jax.experimental import pallas as pl
from jax.experimental.pallas import tpu as pltpu
from jax.sharding import Mesh
from jax.sharding import PartitionSpec as P

HEADS = 8
DEPTH = 32
WIDE = 256
SCALE = DEPTH ** (-0.5)
EPS = 1e-05
DAP = ("dap_0", "dap_1", "dap_2", "dap_3")
MESH = pl.DeviceIdType.MESH
F32 = jnp.float32
BF16 = jnp.bfloat16


def layer_norm(x):
    center = x - jnp.mean(x, axis=-1, keepdims=True)
    spread = jnp.mean(center * center, axis=-1, keepdims=True)
    return center * lax.rsqrt(spread + EPS)


def mm(a, b):
    return jnp.dot(a, b, preferred_element_type=F32)


def plane_id(k):
    return {"dap_1": lax.div(k, 8), "dap_2": lax.rem(lax.div(k, 2), 4), "dap_3": lax.rem(k, 2)}


def kernel(
    hom_h, pair_h, mask_h, chain_h, bproj_h, cbias_h, wh_h, ph_h, wc_h, pv_h, ex_h, co_h,
    out,
    pair, chain, bproj, cbias, wh, ph, wc, pv, ex, co,
    xs, mine, plane, biasall, homall, mrow, mcol, keep, keepc,
    qbd, vt, scores, ot, gt,
    a1, a2s, a2, b1s, b1, b2s, b2, fs,
    lsem, plane_s, plane_r, hom_s, hom_r, mrow_s, mrow_r, mp_s, mp_r, mz_s, mz_r,
    ring_s, ring_r, part_s, part_r, a1_s, a1_r, a2_s, a2_r, b1_s, b1_r, b2_s, b2_r,
):
    z = lax.axis_index("dap_0")
    y = lax.axis_index("dap_1")
    x = lax.axis_index("dap_2")
    c = lax.axis_index("dap_3")
    seq = lax.axis_index("seq")
    k = y * 8 + x * 2 + c
    dap = z * 16 + k

    def local(n, src, dst):
        return pltpu.make_async_copy(src, dst, lsem.at[n])

    l_pair = local(0, pair_h, pair)
    l_chain = local(1, chain_h, chain)
    l_bproj = local(2, bproj_h, bproj)
    l_cbias = local(3, cbias_h, cbias)
    l_hom = local(4, hom_h, homall.at[seq])
    l_mrow = local(5, mask_h, mrow.at[seq])
    l_mcol = local(6, mask_h, mcol.at[z, k])
    l_wh = local(7, wh_h, wh)
    l_rest = [local(8 + n, a, b) for n, (a, b) in enumerate(
        ((ph_h, ph), (wc_h, wc), (pv_h, pv), (ex_h, ex), (co_h, co)))]
    for ld in (l_pair, l_chain, l_bproj, l_cbias, l_hom, l_mrow, l_mcol):
        ld.start()

    def remote(src, dst, ss, rs, device):
        return pltpu.make_async_remote_copy(
            src_ref=src, dst_ref=dst, send_sem=ss, recv_sem=rs, device_id=device,
            device_id_type=MESH)

    barrier = pltpu.get_barrier_semaphore()

    @pl.loop(1, 8)
    def _(p):
        pl.semaphore_signal(barrier, inc=1, device_id={"dap_0": lax.rem(z + p, 8)}, device_id_type=MESH)

    @pl.loop(1, 4)
    def _(p):
        pl.semaphore_signal(barrier, inc=1, device_id={"seq": lax.rem(seq + p, 4)}, device_id_type=MESH)

    @pl.loop(1, 16)
    def _(p):
        pl.semaphore_signal(barrier, inc=1, device_id=plane_id(lax.rem(k + p, 16)), device_id_type=MESH)

    l_wh.start()
    for ld in l_rest:
        ld.start()

    l_chain.wait()
    l_cbias.wait()
    diagonal = (lax.broadcasted_iota(jnp.int32, (8, 8), 0)
                == lax.broadcasted_iota(jnp.int32, (8, 8), 1))

    def by_head(row):
        return jnp.sum(jnp.where(diagonal, jnp.broadcast_to(row, (8, 8)), 0.0), axis=1, keepdims=True)

    cb0 = jnp.broadcast_to(by_head(cbias[0:1, :]), (8, 128))
    cb1 = jnp.broadcast_to(by_head(cbias[1:2, :]), (8, 128))
    row_chain = jnp.broadcast_to(chain[pl.ds(seq, 1), :], (8, 128))
    my_chain = jnp.broadcast_to(chain[pl.ds(lax.div(dap, 32), 1), :], (8, 128))
    lane = lax.broadcasted_iota(jnp.int32, (8, 128), 1) - lax.rem(dap, 32) * 4
    terms = []
    for j in range(4):
        own_chain = jnp.sum(jnp.where(lane == j, my_chain, 0).astype(F32), axis=1, keepdims=True)
        terms.append(jnp.where(row_chain.astype(F32) == own_chain, cb0, cb1))
    with jax.named_scope("waitpair"):
        l_pair.wait()
    xs[...] = layer_norm(pair[...].astype(F32))
    l_bproj.wait()
    parts = []
    for j in range(4):
        xj = xs[pl.ds(j, 128, stride=4), :]
        pj = lax.dot_general(bproj[...], xj, (((1,), (1,)), ((), ())), precision=lax.Precision.HIGHEST,
                             preferred_element_type=F32)
        parts.append(pj + terms[j])
    for g in range(2):
        mine[g] = jnp.concatenate([p[g * 4:g * 4 + 4] for p in parts], axis=0).astype(BF16)
    plane[k] = mine[c]
    l_hom.wait()
    l_mrow.wait()
    l_mcol.wait()
    qbd[...] = jnp.zeros_like(qbd)

    with jax.named_scope("barrier"):
        pl.semaphore_wait(barrier, 25)

    def plane_copy(p):
        to = lax.rem(k + p, 16)
        return remote(mine.at[lax.rem(to, 2)], plane.at[k], plane_s, plane_r, plane_id(to))

    def hom_copy(p):
        to = lax.rem(seq + p, 4)
        return remote(homall.at[seq], homall.at[seq], hom_s, hom_r.at[seq], {"seq": to})

    def hom_recv(p):
        fr = lax.rem(seq + p, 4)
        return remote(homall.at[fr], homall.at[fr], hom_s, hom_r.at[fr], {"seq": fr})

    def mrow_copy(p):
        to = lax.rem(seq + p, 4)
        return remote(mrow.at[seq], mrow.at[seq], mrow_s, mrow_r, {"seq": to})

    def mp_copy(p):
        to = lax.rem(k + p, 16)
        return remote(mcol.at[z, k], mcol.at[z, k], mp_s, mp_r, plane_id(to))

    def mz_copy(p):
        to = lax.rem(z + p, 8)
        return remote(mcol.at[z], mcol.at[z], mz_s, mz_r, {"dap_0": to})

    def drain(ref, sem):
        pltpu.make_async_copy(ref, ref, sem).wait()

    pl.loop(1, 16)(lambda p: plane_copy(p).start())
    pl.loop(1, 4)(lambda p: mrow_copy(p).start())
    pl.loop(1, 16)(lambda p: mp_copy(p).start())
    pl.loop(1, 4)(lambda p: hom_copy(p).start())

    def transposed(v):
        return v.astype(BF16).T

    def spread_queries(qt):
        for h in range(HEADS):
            qbd[h * 32:(h + 1) * 32, h * 128:(h + 1) * 128] = qt[h * 32:(h + 1) * 32, :]

    def block_scores(b, keys, values):
        scores[pl.ds(pl.multiple_of(b * 128, 128), 128), :] = mm(keys.astype(BF16), qbd[...])
        vt[:, pl.ds(pl.multiple_of(b * 128, 128), 128)] = transposed(values)

    l_wh.wait()
    own = homall[seq].astype(F32)
    with jax.named_scope("ownqkv"):
        qkvg = mm(layer_norm(own).astype(BF16), wh[...])
        spread_queries(transposed(qkvg[:, :WIDE]))
        gt[...] = transposed(qkvg[:, 3 * WIDE:]).astype(F32)
        block_scores(seq, qkvg[:, WIDE:2 * WIDE], qkvg[:, 2 * WIDE:3 * WIDE])

    def neighbour_block(p):
        b = lax.rem(seq + p, 4)
        with jax.named_scope(f"hom{p}"):
            hom_recv(p).wait_recv()
        kv = mm(layer_norm(homall[b].astype(F32)).astype(BF16), wh[:, WIDE:3 * WIDE])
        block_scores(b, kv[:, :WIDE], kv[:, WIDE:])

    with jax.named_scope("waitplane"):
        drain(plane.at[pl.ds(0, 15)], plane_r)
    xs[:256, :] = plane[...].reshape(256, 128).astype(F32)
    for h in range(4):
        biasall[c, z, :, h * 128:(h + 1) * 128] = xs[pl.ds(h, 64, stride=4), :].astype(BF16)

    steps = (1, 7)
    partner = {"dap_3": 1 - c}

    def piece(half, block, i):
        return biasall.at[half, block, pl.ds(i * 32, 32)]

    def ring_copy(d, s, i):
        ref = piece(c, lax.rem(z + (8 - steps[d]) * s, 8), i)
        return remote(ref, ref, ring_s, ring_r.at[d, s, i], {"dap_0": lax.rem(z + steps[d], 8)})

    def ring_recv(d, s, i):
        ref = piece(c, lax.rem(z + (8 - steps[d]) * (s + 1), 8), i)
        return remote(ref, ref, ring_s, ring_r.at[d, s, i], {"dap_0": lax.rem(z + steps[d], 8)})

    def part_copy(d, s, i):
        ref = piece(c, lax.rem(z + (8 - steps[d]) * (s + 1), 8), i)
        return remote(ref, ref, part_s, part_r, partner)

    hops = [(d, s, i) for s in range(4) for i in range(2) for d in range(2) if s < 3 or i == d]
    for i in range(2):
        for d in range(2):
            ring_copy(d, 0, i).start()
    remote(biasall.at[c, z], biasall.at[c, z], part_s, part_r, partner).start()
    with jax.named_scope("nb1"):
        neighbour_block(1)
    for d, s, i in hops:
        with jax.named_scope(f"ring{d}{s}{i}"):
            ring_recv(d, s, i).wait_recv()
        if (d, s + 1, i) in hops:
            ring_copy(d, s + 1, i).start()
        part_copy(d, s, i).start()
        if (d, s, i) == (1, 0, 1):
            with jax.named_scope("waitmp"):
                drain(mcol.at[0, pl.ds(0, 15)], mp_r)
            pl.loop(1, 8)(lambda p: mz_copy(p).start())
            with jax.named_scope("nb3"):
                neighbour_block(3)
        if (d, s, i) == (1, 1, 1):
            with jax.named_scope("nb2"):
                neighbour_block(2)
        if (d, s, i) == (1, 2, 0):
            with jax.named_scope("mask"):
                drain(mrow.at[pl.ds(0, 3)], mrow_r)
                for b in range(4):
                    keep[b * 128:(b + 1) * 128, :] = jnp.broadcast_to(mrow[b].astype(F32), (128, 128)).T
                drain(mcol.at[pl.ds(0, 7)], mz_r)
                fs[:128, :] = mcol[...].reshape(128, 128).astype(F32)
                pick = (lax.broadcasted_iota(jnp.int32, (128, 128), 0) == dap).astype(BF16)
                rows = [fs[pl.ds(n, 8, stride=16), :] for n in range(16)]
                keepc[...] = mm(jnp.concatenate(rows, axis=0).astype(BF16), pick)
    with jax.named_scope("partner"):
        drain(biasall.at[1 - c], part_r)

    def softmax_out(s, vth):
        m = jnp.max(s, axis=0, keepdims=True)
        e = jnp.exp(s - m)
        w = (e * (1.0 / jnp.sum(e, axis=0, keepdims=True))).astype(BF16)
        return mm(vth, w)

    with jax.named_scope("rowattn"):
        for h in range(HEADS):
            lanes = slice(h * 128, (h + 1) * 128)
            s = scores[:, lanes] * SCALE + biasall[h // 4, :, :, (h % 4) * 128:(h % 4 + 1) * 128].reshape(512, 128).astype(F32)
            s = jnp.where(keep[...] > 0.0, s, -1000000000.0)
            ot[h * 32:(h + 1) * 32, :] = softmax_out(s, vt[h * 32:(h + 1) * 32, :])

    def split(v):
        fs[:128, :] = v[:, :128].astype(F32)
        fs[128:, :] = v[:, 128:].astype(F32)

    def gated_project(w):
        g = (jax.nn.sigmoid(gt[...]) * ot[...]).astype(BF16)
        return mm(g.T, w)

    with jax.named_scope("rowproj"):
        l_rest[0].wait()
        one = (homall[seq].astype(F32) + gated_project(ph[...])).astype(BF16)
        b2s[...] = one.reshape(8, 16, WIDE)
        a1[z] = b2s[z]

    def a1_copy(p):
        to = lax.rem(z + p, 8)
        return remote(b2s.at[to], a1.at[z], a1_s, a1_r, {"dap_0": to})

    pl.loop(1, 8)(lambda p: a1_copy(p).start())
    with jax.named_scope("waita1"):
        drain(a1.at[pl.ds(0, 7)], a1_r)

    split(a1[...].reshape(128, WIDE))
    for n in range(16):
        for t in range(2):
            a2s[n, :, t * 128:(t + 1) * 128] = fs[pl.ds(t * 128 + n, 8, stride=16), :].astype(BF16)
    a2[k] = a2s[k]

    def a2_copy(p):
        to = lax.rem(k + p, 16)
        return remote(a2s.at[to], a2.at[k], a2_s, a2_r, plane_id(to))

    pl.loop(1, 16)(lambda p: a2_copy(p).start())
    for ld in l_rest[1:]:
        ld.wait()
    with jax.named_scope("waita2"):
        drain(a2.at[pl.ds(0, 15)], a2_r)

    with jax.named_scope("colattn"):
        col = a2[...].astype(F32).reshape(128, WIDE)
        qkvg = mm(layer_norm(col).astype(BF16), wc[...])
        spread_queries(transposed(qkvg[:, :WIDE]))
        gt[...] = transposed(qkvg[:, 3 * WIDE:]).astype(F32)
        cs = mm(qkvg[:, WIDE:2 * WIDE].astype(BF16), qbd[...]) * SCALE
        cvt = transposed(qkvg[:, 2 * WIDE:3 * WIDE])
        for h in range(HEADS):
            s = jnp.where(keepc[...] > 0.0, cs[:, h * 128:(h + 1) * 128], -1000000000.0)
            ot[h * 32:(h + 1) * 32, :] = softmax_out(s, cvt[h * 32:(h + 1) * 32, :])
    with jax.named_scope("transition"):
        two = col + gated_project(pv[...])
        inner = jnp.maximum(mm(layer_norm(two).astype(BF16), ex[...]), 0.0).astype(BF16)
        done = two + mm(inner, co[...])
        b1s[...] = done.reshape(16, 8, WIDE).astype(BF16)
        b1[k] = b1s[k]

    def b1_copy(p):
        to = lax.rem(k + p, 16)
        return remote(b1s.at[to], b1.at[k], b1_s, b1_r, plane_id(to))

    pl.loop(1, 16)(lambda p: b1_copy(p).start())
    drain(a1.at[pl.ds(0, 7)], a1_s)
    with jax.named_scope("waitb1"):
        drain(b1.at[pl.ds(0, 15)], b1_r)
    split(b1[...].astype(F32).reshape(128, WIDE))
    for n in range(8):
        for t in range(2):
            b2s[n, :, t * 128:(t + 1) * 128] = fs[pl.ds(t * 128 + n, 16, stride=8), :].astype(BF16)
    b2[z] = b2s[z]

    def b2_copy(p):
        to = lax.rem(z + p, 8)
        return remote(b2s.at[to], b2.at[z], b2_s, b2_r, {"dap_0": to})

    pl.loop(1, 8)(lambda p: b2_copy(p).start())

    drain(plane.at[pl.ds(0, 15)], plane_s)
    drain(mcol.at[0, pl.ds(0, 15)], mp_s)
    drain(a2.at[pl.ds(0, 15)], a2_s)
    drain(b1.at[pl.ds(0, 15)], b1_s)
    drain(mcol.at[pl.ds(0, 7)], mz_s)
    drain(homall.at[pl.ds(0, 3)], hom_s)
    drain(mrow.at[pl.ds(0, 3)], mrow_s)
    drain(biasall.at[0, pl.ds(0, 7)], ring_s)
    drain(biasall.at[0], part_s)
    with jax.named_scope("waitb2"):
        drain(b2.at[pl.ds(0, 7)], b2_r)
    with jax.named_scope("tail"):
        drain(b2.at[pl.ds(0, 7)], b2_s)
        out[...] = b2[...].reshape(128, WIDE)


def body(
    homolog_tensor, pair_features, entry_real_mask, chain_ids, horizontal_matrices,
    horizontal_projector, bias_proj, chain_bias, column_proj, vertical_projector,
    expansion_matrix, contraction_matrix,
):
    vmem = pl.BlockSpec(memory_space=pltpu.VMEM)
    hbm = pl.BlockSpec(memory_space=pl.ANY)
    dma = pltpu.SemaphoreType.DMA
    updated = pl.pallas_call(
        kernel,
        name="msa_block",
        out_shape=pltpu.VMEM((128, WIDE), BF16),
        in_specs=[hbm] * 12,
        out_specs=vmem,
        scratch_shapes=[
            pltpu.VMEM((512, 128), BF16),
            pltpu.VMEM((4, 128), jnp.int32),
            pltpu.VMEM((8, 128), F32),
            pltpu.VMEM((2, 8), F32),
            pltpu.VMEM((WIDE, 4 * WIDE), BF16),
            pltpu.VMEM((WIDE, WIDE), BF16),
            pltpu.VMEM((WIDE, 4 * WIDE), BF16),
            pltpu.VMEM((WIDE, WIDE), BF16),
            pltpu.VMEM((WIDE, 4 * WIDE), BF16),
            pltpu.VMEM((4 * WIDE, WIDE), BF16),
            pltpu.VMEM((512, 128), F32),
            pltpu.VMEM((2, 16, 128), BF16),
            pltpu.VMEM((16, 16, 128), BF16),
            pltpu.VMEM((2, 8, 64, 512), BF16),
            pltpu.VMEM((4, 128, WIDE), BF16),
            pltpu.VMEM((4, 1, 128), jnp.int32),
            pltpu.VMEM((8, 16, 1, 128), jnp.int32),
            pltpu.VMEM((512, 128), F32),
            pltpu.VMEM((128, 128), F32),
            pltpu.VMEM((WIDE, 1024), BF16),
            pltpu.VMEM((WIDE, 512), BF16),
            pltpu.VMEM((512, 1024), F32),
            pltpu.VMEM((WIDE, 128), F32),
            pltpu.VMEM((WIDE, 128), F32),
            pltpu.VMEM((8, 16, WIDE), BF16),
            pltpu.VMEM((16, 8, WIDE), BF16),
            pltpu.VMEM((16, 8, WIDE), BF16),
            pltpu.VMEM((16, 8, WIDE), BF16),
            pltpu.VMEM((16, 8, WIDE), BF16),
            pltpu.VMEM((8, 16, WIDE), BF16),
            pltpu.VMEM((8, 16, WIDE), BF16),
            pltpu.VMEM((256, 128), F32),
            dma((13,)), dma, dma, dma, dma((4,)), dma, dma, dma, dma, dma, dma,
            dma, dma((2, 4, 2)), dma, dma, dma, dma, dma, dma, dma, dma, dma, dma,
        ],
        compiler_params=pltpu.CompilerParams(collective_id=0, has_side_effects=True),
    )(
        homolog_tensor.reshape(128, WIDE),
        pair_features.reshape(512, 128),
        entry_real_mask,
        chain_ids.reshape(4, 128),
        bias_proj.T,
        chain_bias,
        horizontal_matrices,
        horizontal_projector,
        column_proj,
        vertical_projector,
        expansion_matrix,
        contraction_matrix,
    )
    return updated.reshape(1, 128, WIDE)


def solution(mesh):
    torus = Mesh(
        mesh.devices.reshape(8, 2, 4, 2, mesh.shape["seq"]),
        ("dap_0", "dap_1", "dap_2", "dap_3", "seq"),
    )
    return jax.shard_map(
        body,
        mesh=torus,
        in_specs=(P(DAP, "seq", None), P("seq", DAP, None), P(DAP, "seq")) + (P(),) * 9,
        out_specs=P(DAP, "seq", None),
        check_vma=False,
    )
```

time: 65 us -> 56.3 us (0.87)
  Pallas kernels: 61.3 us -> 55.1 us
  local copies, waits for them, and re-layouts: 3.48 us -> 0.63 us
    pallas_call x1, Pallas kernels: 61.3 us -> 55.1 us  [body(): pl.pallas_call(kernel, name='msa_block', out_shape=pltpu.VMEM((128, WIDE)...]
    unnamed x6 -> x1, local copies, waits for them, and re-layouts: 2.9 us -> 0.63 us
where the time goes in v2:
time: 56.3 us; the launch traced here: 55.7 us
  Pallas kernels  55.1 us (98%)
  local copies, waits for them, and re-layouts  0.63 us (1%)
    pallas_call x1, Pallas kernels, body(): pl.pallas_call(kernel, name='msa_block', out_shape=pltpu.VMEM((128, WIDE)...  55.1 us

profile of v2, /device:TPU:1, one launch (start us, length us, event | category | flops | bytes accessed | tf_op | source)
XLA Modules:
  0.0 55.7 jit_solution(14209687596157442836)
XLA Ops:
  0.0 55.1 %msa_block.1 = bf16[128,256]{1,0:T(8,128)(2,1)S(1)} custom-call(bf16[128,256]{1,0:T(8,128)(2,1)} %bitcast.7, bf16[512,128]{1,0:T(8,128)(2,1)} %bitcast.6, s32[1,128]{1,0:T(1,128)} %mask_h.1, s32[4,128]{1,0:T(4,128)} %bitcast.9, f32[8,128]{1,0:T(8,128)} %bitcast.8, f32[2,8]{1,0:T(2,128)} %cbias_h.1, bf16[256,1024]{1,0:T(8,128)(2,1)} %wh_h.1, ...), custom_call_target="tpu_custom_call" | custom-call | tf_op jit(solution)/shard_map/msa_block/pallas_call | solution.py:358
  55.1 0.6 %copy.14 = bf16[1,128,256]{2,1,0:T(8,128)(2,1)} copy(bf16[1,128,256]{2,1,0:T(8,128)(2,1)S(1)} %bitcast.5) | data formatting | bytes 131072

commit v3 on v2

v3 whole, which is shorter than its diff:
```python
import jax
import jax.numpy as jnp
from jax import lax
from jax.experimental import pallas as pl
from jax.experimental.pallas import tpu as pltpu
from jax.sharding import Mesh
from jax.sharding import PartitionSpec as P

HEADS = 8
DEPTH = 32
WIDE = 256
SCALE = DEPTH ** (-0.5)
EPS = 1e-05
DAP = ("dap_0", "dap_1", "dap_2", "dap_3")
MESH = pl.DeviceIdType.MESH
F32 = jnp.float32
BF16 = jnp.bfloat16


def layer_norm(x):
    center = x - jnp.mean(x, axis=-1, keepdims=True)
    spread = jnp.mean(center * center, axis=-1, keepdims=True)
    return center * lax.rsqrt(spread + EPS)


def mm(a, b):
    return jnp.dot(a, b, preferred_element_type=F32)


def far_id(g):
    return {"dap_0": lax.div(g, 2), "dap_1": lax.rem(g, 2)}


def near_id(q):
    return {"dap_2": lax.div(q, 2), "dap_3": lax.rem(q, 2)}


def kernel(
    hom_h, pair_h, mask_h, chain_h, bproj_h, cbias_h, wh_h, ph_h, wc_h, pv_h, ex_h, co_h,
    out,
    pair, chain, bproj, cbias, wh, ph, wc, pv, ex, co,
    xs, mine, zbuf, pack, biasall, homall, mrow, mzb, mcol, keep, keepc,
    qbd, vrow, vt, scores, ot, gt,
    a1s, a1, a2s, a2, b1s, b1, b2s, b2, fs,
    lsem, z_s, z_r, hom_s, hom_r, mrow_s, mrow_r, mp_s, mp_r, mz_s, mz_r,
    wave_s, wave_r, part_s, part_r, a1_s, a1_r, a2_s, a2_r, b1_s, b1_r, b2_s, b2_r,
):
    z = lax.axis_index("dap_0")
    y = lax.axis_index("dap_1")
    x = lax.axis_index("dap_2")
    c = lax.axis_index("dap_3")
    seq = lax.axis_index("seq")
    g = z * 2 + y
    q = x * 2 + c
    dap = g * 8 + q

    def local(n, src, dst):
        return pltpu.make_async_copy(src, dst, lsem.at[n])

    l_pair = local(0, pair_h, pair)
    l_chain = local(1, chain_h, chain)
    l_bproj = local(2, bproj_h, bproj)
    l_cbias = local(3, cbias_h, cbias)
    l_hom = local(4, hom_h, homall.at[seq])
    l_mrow = local(5, mask_h, mrow.at[seq])
    l_mcol = local(6, mask_h, mzb.at[g])
    l_wh = local(7, wh_h, wh)
    l_rest = [local(8 + n, a, b) for n, (a, b) in enumerate(
        ((ph_h, ph), (wc_h, wc), (pv_h, pv), (ex_h, ex), (co_h, co)))]
    for ld in (l_pair, l_chain, l_bproj, l_cbias, l_hom, l_mrow, l_mcol):
        ld.start()

    def remote(src, dst, ss, rs, device):
        return pltpu.make_async_remote_copy(
            src_ref=src, dst_ref=dst, send_sem=ss, recv_sem=rs, device_id=device,
            device_id_type=MESH)

    barrier = pltpu.get_barrier_semaphore()

    @pl.loop(1, 16)
    def _(p):
        pl.semaphore_signal(barrier, inc=1, device_id=far_id(lax.rem(g + p, 16)), device_id_type=MESH)

    @pl.loop(1, 4)
    def _(p):
        pl.semaphore_signal(barrier, inc=1, device_id={"seq": lax.rem(seq + p, 4)}, device_id_type=MESH)

    @pl.loop(1, 8)
    def _(p):
        pl.semaphore_signal(barrier, inc=1, device_id=near_id(lax.rem(q + p, 8)), device_id_type=MESH)

    l_wh.start()
    for ld in l_rest:
        ld.start()

    l_chain.wait()
    l_cbias.wait()
    diagonal = (lax.broadcasted_iota(jnp.int32, (8, 8), 0)
                == lax.broadcasted_iota(jnp.int32, (8, 8), 1))

    def by_head(row):
        return jnp.sum(jnp.where(diagonal, jnp.broadcast_to(row, (8, 8)), 0.0), axis=1, keepdims=True)

    cb0 = jnp.broadcast_to(by_head(cbias[0:1, :]), (8, 128))
    cb1 = jnp.broadcast_to(by_head(cbias[1:2, :]), (8, 128))
    row_chain = jnp.broadcast_to(chain[pl.ds(seq, 1), :], (8, 128))
    my_chain = jnp.broadcast_to(chain[pl.ds(lax.div(dap, 32), 1), :], (8, 128))
    lane = lax.broadcasted_iota(jnp.int32, (8, 128), 1) - lax.rem(dap, 32) * 4
    terms = []
    for j in range(4):
        own_chain = jnp.sum(jnp.where(lane == j, my_chain, 0).astype(F32), axis=1, keepdims=True)
        terms.append(jnp.where(row_chain.astype(F32) == own_chain, cb0, cb1))
    with jax.named_scope("waitpair"):
        l_pair.wait()
    xs[...] = layer_norm(pair[...].astype(F32))
    l_bproj.wait()
    parts = []
    for j in range(4):
        xj = xs[pl.ds(j, 128, stride=4), :]
        pj = lax.dot_general(bproj[...], xj, (((1,), (1,)), ((), ())), precision=lax.Precision.HIGHEST,
                             preferred_element_type=F32)
        parts.append(pj + terms[j])
    mine[...] = jnp.concatenate(parts, axis=0).astype(BF16)
    zbuf[g] = mine[...]
    l_hom.wait()
    l_mrow.wait()
    l_mcol.wait()
    qbd[...] = jnp.zeros_like(qbd)

    with jax.named_scope("barrier"):
        pl.semaphore_wait(barrier, 25)

    def z_copy(p):
        to = lax.rem(g + p, 16)
        return remote(mine, zbuf.at[g], z_s, z_r.at[lax.div(z, 4)], far_id(to))

    def hom_copy(p):
        to = lax.rem(seq + p, 4)
        return remote(homall.at[seq], homall.at[seq], hom_s, hom_r.at[seq], {"seq": to})

    def hom_recv(p):
        fr = lax.rem(seq + p, 4)
        return remote(homall.at[fr], homall.at[fr], hom_s, hom_r.at[fr], {"seq": fr})

    def mrow_copy(p):
        to = lax.rem(seq + p, 4)
        return remote(mrow.at[seq], mrow.at[seq], mrow_s, mrow_r, {"seq": to})

    def mz_copy(p):
        to = lax.rem(g + p, 16)
        return remote(mzb.at[g], mzb.at[g], mz_s, mz_r, far_id(to))

    def mp_copy(p):
        to = lax.rem(q + p, 8)
        return remote(mzb, mcol.at[q], mp_s, mp_r, near_id(to))

    def drain(ref, sem):
        pltpu.make_async_copy(ref, ref, sem).wait()

    pl.loop(1, 16)(lambda p: z_copy(p).start())
    pl.loop(1, 4)(lambda p: hom_copy(p).start())
    pl.loop(1, 16)(lambda p: mz_copy(p).start())
    pl.loop(1, 4)(lambda p: mrow_copy(p).start())

    def transposed(v):
        return v.astype(BF16).T

    def spread_queries(qt):
        for h in range(HEADS):
            qbd[h * 32:(h + 1) * 32, h * 128:(h + 1) * 128] = qt[h * 32:(h + 1) * 32, :]

    ri = lax.broadcasted_iota(jnp.int32, (128, 128), 0)
    ci = lax.broadcasted_iota(jnp.int32, (128, 128), 1)
    source = ((ri >> 3) & 1) * 64 + ((ri >> 2) & 1) * 32 + (ri >> 4) * 4 + (ri & 3)
    order = (ci == source).astype(BF16)

    def ordered(v):
        return mm(order, v).astype(BF16)

    def place(ref, b, v):
        rows = pl.ds(pl.multiple_of(lax.rem(b, 2) * 16, 16), 16)
        ref[lax.div(b, 2), :, rows, :] = v.reshape(8, 16, v.shape[-1])

    def block_scores(b, keys, values):
        place(scores, b, mm(keys.astype(BF16), qbd[...]))
        place(vrow, b, values)

    l_wh.wait()
    own = homall[seq].astype(F32)
    with jax.named_scope("ownqkv"):
        normed = layer_norm(own).astype(BF16)
        qg = mm(normed, wh[...])
        spread_queries(transposed(qg[:, :WIDE]))
        gt[...] = transposed(qg[:, 3 * WIDE:]).astype(F32)
        kv = mm(ordered(normed), wh[:, WIDE:3 * WIDE])
        block_scores(seq, kv[:, :WIDE], kv[:, WIDE:])

    def neighbour_block(p):
        b = lax.rem(seq + p, 4)
        with jax.named_scope(f"hom{p}"):
            hom_recv(p).wait_recv()
        kv = mm(ordered(layer_norm(homall[b].astype(F32)).astype(BF16)), wh[:, WIDE:3 * WIDE])
        block_scores(b, kv[:, :WIDE], kv[:, WIDE:])

    partner = {"dap_3": 1 - c}

    def wave_copy(e, p):
        to = lax.rem(q + p, 8)
        half = lax.rem(to, 2)
        return remote(pack.at[e, half], biasall.at[half, e, q], wave_s.at[e], wave_r.at[e], near_id(to))

    first = lax.div(z, 4)
    second = 1 - first

    def wave_send(e, count):
        with jax.named_scope(f"zwait{count}"):
            drain(zbuf.at[pl.ds(0, count)], z_r.at[e])
        xs[:256, :] = zbuf[pl.ds(e * 8, 8)].reshape(256, 128).astype(F32)
        for h in range(HEADS):
            pack[e, h // 4, :, (h % 4) * 128:(h % 4 + 1) * 128] = xs[pl.ds(h, 32, stride=8), :].astype(BF16)
        biasall[c, e, q] = pack[e, c]
        pl.loop(1, 8)(lambda p: wave_copy(e, p).start())

    def hand_over(e, n):
        with jax.named_scope(f"wave{n}"):
            drain(biasall.at[0, 0, pl.ds(0, 7)], wave_r.at[e])
        remote(biasall.at[c, e], biasall.at[c, e], part_s, part_r, partner).start()

    wave_send(first, 7)
    wave_send(second, 8)
    with jax.named_scope("nb1"):
        neighbour_block(1)
    with jax.named_scope("nb3"):
        neighbour_block(3)
    hand_over(first, 0)
    with jax.named_scope("nb2"):
        neighbour_block(2)
    with jax.named_scope("mask"):
        vt[...] = vrow[...].reshape(512, WIDE).astype(BF16).T
        drain(mrow.at[pl.ds(0, 3)], mrow_r)
        for b in range(4):
            place(keep, b, mm(order, jnp.broadcast_to(mrow[b].astype(F32), (128, 128)).T.astype(BF16)))
        drain(mzb.at[pl.ds(0, 15)], mz_r)
    pl.loop(1, 8)(lambda p: mp_copy(p).start())
    mcol[q] = mzb[...]
    hand_over(second, 1)

    def softmax_out(s, vth):
        m = jnp.max(s, axis=0, keepdims=True)
        e = jnp.exp(s - m)
        w = (e * (1.0 / jnp.sum(e, axis=0, keepdims=True))).astype(BF16)
        return mm(vth, w)

    def row_head(half, h):
        head = half * 4 + h
        lanes = pl.ds(pl.multiple_of(head * 128, 128), 128)
        rows = pl.ds(pl.multiple_of(head * 32, 32), 32)
        s = scores[:, :, :, lanes].reshape(512, 128) * SCALE
        s = s + biasall[half, :, :, :, h * 128:(h + 1) * 128].reshape(512, 128).astype(F32)
        s = jnp.where(keep[...].reshape(512, 128) > 0.0, s, -1000000000.0)
        ot[rows, :] = softmax_out(s, vt[rows, :])

    with jax.named_scope("rowattn"):
        for h in range(4):
            row_head(c, h)
    with jax.named_scope("partner"):
        drain(biasall.at[1 - c], part_r)
    with jax.named_scope("rowattn2"):
        for h in range(4):
            row_head(1 - c, h)

    def split(v):
        fs[:128, :] = v[:, :128].astype(F32)
        fs[128:, :] = v[:, 128:].astype(F32)

    def gated_project(w):
        g = (jax.nn.sigmoid(gt[...]) * ot[...]).astype(BF16)
        return mm(g.T, w)

    with jax.named_scope("rowproj"):
        l_rest[0].wait()
        one = (homall[seq].astype(F32) + gated_project(ph[...])).astype(BF16).astype(F32)
        a1s[...] = one.reshape(16, 8, WIDE).astype(BF16)
        a1[g] = a1s[g]

    def a1_copy(p):
        to = lax.rem(g + p, 16)
        return remote(a1s.at[to], a1.at[g], a1_s, a1_r, far_id(to))

    pl.loop(1, 16)(lambda p: a1_copy(p).start())
    with jax.named_scope("waita1"):
        drain(a1.at[pl.ds(0, 15)], a1_r)

    split(a1[...].astype(F32).reshape(128, WIDE))
    for n in range(8):
        for t in range(2):
            a2s[n, :, t * 128:(t + 1) * 128] = fs[pl.ds(t * 128 + n, 16, stride=8), :].astype(BF16)
    a2[q] = a2s[q]

    def a2_copy(p):
        to = lax.rem(q + p, 8)
        return remote(a2s.at[to], a2.at[q], a2_s, a2_r, near_id(to))

    pl.loop(1, 8)(lambda p: a2_copy(p).start())
    for ld in l_rest[1:]:
        ld.wait()
    with jax.named_scope("keepc"):
        drain(mcol.at[pl.ds(0, 7)], mp_r)
        pick = (ri == dap).astype(BF16)
        keepc[...] = mm(mcol[...].reshape(128, 128).astype(F32).astype(BF16), pick)
    with jax.named_scope("waita2"):
        drain(a2.at[pl.ds(0, 7)], a2_r)

    with jax.named_scope("colattn"):
        col = a2[...].reshape(128, WIDE).astype(F32)
        qkvg = mm(layer_norm(col).astype(BF16), wc[...])
        spread_queries(transposed(qkvg[:, :WIDE]))
        gt[...] = transposed(qkvg[:, 3 * WIDE:]).astype(F32)
        cs = mm(qkvg[:, WIDE:2 * WIDE].astype(BF16), qbd[...]) * SCALE
        cvt = transposed(qkvg[:, 2 * WIDE:3 * WIDE])
        for h in range(HEADS):
            s = jnp.where(keepc[...] > 0.0, cs[:, h * 128:(h + 1) * 128], -1000000000.0)
            ot[h * 32:(h + 1) * 32, :] = softmax_out(s, cvt[h * 32:(h + 1) * 32, :])
    with jax.named_scope("transition"):
        two = col + gated_project(pv[...])
        inner = jnp.maximum(mm(layer_norm(two).astype(BF16), ex[...]), 0.0).astype(BF16)
        done = two + mm(inner, co[...])
        b1s[...] = done.astype(BF16).reshape(8, 16, WIDE)
        b1[q] = b1s[q]

    def b1_copy(p):
        to = lax.rem(q + p, 8)
        return remote(b1s.at[to], b1.at[q], b1_s, b1_r, near_id(to))

    pl.loop(1, 8)(lambda p: b1_copy(p).start())
    with jax.named_scope("waitb1"):
        drain(b1.at[pl.ds(0, 7)], b1_r)
    split(b1[...].reshape(128, WIDE))
    for n in range(16):
        for t in range(2):
            b2s[n, :, t * 128:(t + 1) * 128] = fs[pl.ds(t * 128 + n, 8, stride=16), :].astype(BF16)
    b2[g] = b2s[g]

    def b2_copy(p):
        to = lax.rem(g + p, 16)
        return remote(b2s.at[to], b2.at[g], b2_s, b2_r, far_id(to))

    pl.loop(1, 16)(lambda p: b2_copy(p).start())

    drain(zbuf.at[pl.ds(0, 15)], z_s)
    for e in range(2):
        drain(biasall.at[0, 0, pl.ds(0, 7)], wave_s.at[e])
    drain(mcol.at[pl.ds(0, 7)], mp_s)
    drain(a1.at[pl.ds(0, 15)], a1_s)
    drain(a2.at[pl.ds(0, 7)], a2_s)
    drain(b1.at[pl.ds(0, 7)], b1_s)
    drain(mzb.at[pl.ds(0, 15)], mz_s)
    drain(homall.at[pl.ds(0, 3)], hom_s)
    drain(mrow.at[pl.ds(0, 3)], mrow_s)
    drain(biasall.at[0], part_s)
    with jax.named_scope("waitb2"):
        drain(b2.at[pl.ds(0, 15)], b2_r)
    drain(b2.at[pl.ds(0, 15)], b2_s)
    out[...] = b2[...].astype(F32).reshape(128, WIDE).astype(BF16)


def body(
    homolog_tensor, pair_features, entry_real_mask, chain_ids, horizontal_matrices,
    horizontal_projector, bias_proj, chain_bias, column_proj, vertical_projector,
    expansion_matrix, contraction_matrix,
):
    vmem = pl.BlockSpec(memory_space=pltpu.VMEM)
    hbm = pl.BlockSpec(memory_space=pl.ANY)
    dma = pltpu.SemaphoreType.DMA
    updated = pl.pallas_call(
        kernel,
        name="msa_block",
        out_shape=pltpu.VMEM((128, WIDE), BF16),
        in_specs=[hbm] * 12,
        out_specs=vmem,
        scratch_shapes=[
            pltpu.VMEM((512, 128), BF16),
            pltpu.VMEM((4, 128), jnp.int32),
            pltpu.VMEM((8, 128), F32),
            pltpu.VMEM((2, 8), F32),
            pltpu.VMEM((WIDE, 4 * WIDE), BF16),
            pltpu.VMEM((WIDE, WIDE), BF16),
            pltpu.VMEM((WIDE, 4 * WIDE), BF16),
            pltpu.VMEM((WIDE, WIDE), BF16),
            pltpu.VMEM((WIDE, 4 * WIDE), BF16),
            pltpu.VMEM((4 * WIDE, WIDE), BF16),
            pltpu.VMEM((512, 128), F32),
            pltpu.VMEM((32, 128), BF16),
            pltpu.VMEM((16, 32, 128), BF16),
            pltpu.VMEM((2, 2, 32, 512), BF16),
            pltpu.VMEM((2, 2, 8, 32, 512), BF16),
            pltpu.VMEM((4, 128, WIDE), BF16),
            pltpu.VMEM((4, 1, 128), jnp.int32),
            pltpu.VMEM((16, 1, 128), jnp.int32),
            pltpu.VMEM((8, 16, 1, 128), jnp.int32),
            pltpu.VMEM((2, 8, 32, 128), F32),
            pltpu.VMEM((128, 128), F32),
            pltpu.VMEM((WIDE, 1024), BF16),
            pltpu.VMEM((2, 8, 32, WIDE), F32),
            pltpu.VMEM((WIDE, 512), BF16),
            pltpu.VMEM((2, 8, 32, 1024), F32),
            pltpu.VMEM((WIDE, 128), F32),
            pltpu.VMEM((WIDE, 128), F32),
            pltpu.VMEM((16, 8, WIDE), BF16),
            pltpu.VMEM((16, 8, WIDE), BF16),
            pltpu.VMEM((8, 16, WIDE), BF16),
            pltpu.VMEM((8, 16, WIDE), BF16),
            pltpu.VMEM((8, 16, WIDE), BF16),
            pltpu.VMEM((8, 16, WIDE), BF16),
            pltpu.VMEM((16, 8, WIDE), BF16),
            pltpu.VMEM((16, 8, WIDE), BF16),
            pltpu.VMEM((256, 128), F32),
            dma((13,)), dma, dma((2,)), dma, dma((4,)), dma, dma, dma, dma, dma, dma,
            dma((2,)), dma((2,)), dma, dma, dma, dma, dma, dma, dma, dma, dma, dma,
        ],
        compiler_params=pltpu.CompilerParams(collective_id=0, has_side_effects=True),
    )(
        homolog_tensor.reshape(128, WIDE),
        pair_features.reshape(512, 128),
        entry_real_mask,
        chain_ids.reshape(4, 128),
        bias_proj.T,
        chain_bias,
        horizontal_matrices,
        horizontal_projector,
        column_proj,
        vertical_projector,
        expansion_matrix,
        contraction_matrix,
    )
    return updated.reshape(1, 128, WIDE)


def solution(mesh):
    torus = Mesh(
        mesh.devices.reshape(8, 2, 4, 2, mesh.shape["seq"]),
        ("dap_0", "dap_1", "dap_2", "dap_3", "seq"),
    )
    return jax.shard_map(
        body,
        mesh=torus,
        in_specs=(P(DAP, "seq", None), P("seq", DAP, None), P(DAP, "seq")) + (P(),) * 9,
        out_specs=P(DAP, "seq", None),
        check_vma=False,
    )
```

time: 56.3 us -> 50 us (0.89)
  Pallas kernels: 55.1 us -> 49.3 us
    pallas_call x1, Pallas kernels: 55.1 us -> 49.3 us  [body(): pl.pallas_call(kernel, name='msa_block', out_shape=pltpu.VMEM((128, WIDE)...]
where the time goes in v3:
time: 50 us; the launch traced here: 49.9 us
  Pallas kernels  49.3 us (99%)
  local copies, waits for them, and re-layouts  0.63 us (1%)
    pallas_call x1, Pallas kernels, body(): pl.pallas_call(kernel, name='msa_block', out_shape=pltpu.VMEM((128, WIDE)...  49.3 us

profile of v3, /device:TPU:1, one launch (start us, length us, event | category | flops | bytes accessed | tf_op | source)
XLA Modules:
  0.0 49.9 jit_solution(14475073360487995173)
XLA Ops:
  0.0 49.3 %msa_block.1 = bf16[128,256]{1,0:T(8,128)(2,1)S(1)} custom-call(bf16[128,256]{1,0:T(8,128)(2,1)} %bitcast.7, bf16[512,128]{1,0:T(8,128)(2,1)} %bitcast.6, s32[1,128]{1,0:T(1,128)} %mask_h.1, s32[4,128]{1,0:T(4,128)} %bitcast.9, f32[8,128]{1,0:T(8,128)} %bitcast.8, f32[2,8]{1,0:T(2,128)} %cbias_h.1, bf16[256,1024]{1,0:T(8,128)(2,1)} %wh_h.1, ...), custom_call_target="tpu_custom_call" | custom-call | tf_op jit(solution)/shard_map/msa_block/pallas_call | solution.py:375
  49.3 0.6 %copy.14 = bf16[1,128,256]{2,1,0:T(8,128)(2,1)} copy(bf16[1,128,256]{2,1,0:T(8,128)(2,1)S(1)} %bitcast.5) | data formatting | bytes 131072

commit v4 on v3

--- a/solution.py
+++ b/solution.py
@@ -27,23 +27,21 @@
     return jnp.dot(a, b, preferred_element_type=F32)
 
 
-def far_id(g):
-    return {"dap_0": lax.div(g, 2), "dap_1": lax.rem(g, 2)}
-
-
-def near_id(q):
-    return {"dap_2": lax.div(q, 2), "dap_3": lax.rem(q, 2)}
+FAR = tuple((dz, dy) for dz in (4, 3, 5, 2, 6, 1, 7, 0) for dy in (1, 0) if dz or dy)
+HALVES = tuple((o, i, dy) for o in range(2) for i in (1, 3, 2, 0) for dy in range(2) if o or i or dy)
+ALL = tuple((dx, dy, dc) for dx in (2, 1, 3, 0) for dy in (1, 0) for dc in (1, 0))
+NEAR = tuple((dx, dc) for dx in (2, 1, 3, 0) for dc in (1, 0) if dx or dc)
 
 
 def kernel(
     hom_h, pair_h, mask_h, chain_h, bproj_h, cbias_h, wh_h, ph_h, wc_h, pv_h, ex_h, co_h,
     out,
     pair, chain, bproj, cbias, wh, ph, wc, pv, ex, co,
-    xs, mine, zbuf, pack, biasall, homall, mrow, mzb, mcol, keep, keepc,
+    xs, mine, zbuf, pack, biasall, homall, mrow, mzb, mcol, keepc,
     qbd, vrow, vt, scores, ot, gt,
-    a1s, a1, a2s, a2, b1s, b1, b2s, b2, fs,
+    a1s, a1, b1s, b2, fs,
     lsem, z_s, z_r, hom_s, hom_r, mrow_s, mrow_r, mp_s, mp_r, mz_s, mz_r,
-    wave_s, wave_r, part_s, part_r, a1_s, a1_r, a2_s, a2_r, b1_s, b1_r, b2_s, b2_r,
+    wave_s, wave_r, part_s, part_r, a1_s, a1_r, b2_s, b2_r,
 ):
     z = lax.axis_index("dap_0")
     y = lax.axis_index("dap_1")
@@ -67,7 +65,7 @@
     l_wh = local(7, wh_h, wh)
     l_rest = [local(8 + n, a, b) for n, (a, b) in enumerate(
         ((ph_h, ph), (wc_h, wc), (pv_h, pv), (ex_h, ex), (co_h, co)))]
-    for ld in (l_pair, l_chain, l_bproj, l_cbias, l_hom, l_mrow, l_mcol):
+    for ld in (l_pair, l_chain, l_cbias, l_bproj):
         ld.start()
 
     def remote(src, dst, ss, rs, device):
@@ -77,18 +75,24 @@
 
     barrier = pltpu.get_barrier_semaphore()
 
-    @pl.loop(1, 16)
-    def _(p):
-        pl.semaphore_signal(barrier, inc=1, device_id=far_id(lax.rem(g + p, 16)), device_id_type=MESH)
-
-    @pl.loop(1, 4)
-    def _(p):
-        pl.semaphore_signal(barrier, inc=1, device_id={"seq": lax.rem(seq + p, 4)}, device_id_type=MESH)
-
-    @pl.loop(1, 8)
-    def _(p):
-        pl.semaphore_signal(barrier, inc=1, device_id=near_id(lax.rem(q + p, 8)), device_id_type=MESH)
-
+    def far(n):
+        zz, yy = lax.rem(z + n[0], 8), lax.rem(y + n[1], 2)
+        return zz * 2 + yy, {"dap_0": zz, "dap_1": yy}
+
+    def near(n):
+        xx, cc = lax.rem(x + n[0], 4), lax.rem(c + n[1], 2)
+        return xx * 2 + cc, {"dap_2": xx, "dap_3": cc}
+
+    with jax.named_scope("signals"):
+        for n in FAR:
+            pl.semaphore_signal(barrier, inc=1, device_id=far(n)[1], device_id_type=MESH)
+        for n in (2, 1, 3):
+            pl.semaphore_signal(barrier, inc=1, device_id={"seq": lax.rem(seq + n, 4)}, device_id_type=MESH)
+        for n in NEAR:
+            pl.semaphore_signal(barrier, inc=1, device_id=near(n)[1], device_id_type=MESH)
+
+    for ld in (l_hom, l_mrow, l_mcol):
+        ld.start()
     l_wh.start()
     for ld in l_rest:
         ld.start()
@@ -114,12 +118,19 @@
         l_pair.wait()
     xs[...] = layer_norm(pair[...].astype(F32))
     l_bproj.wait()
+    w_top = bproj[...].astype(BF16).astype(F32)
+    w_both = jnp.concatenate([w_top, bproj[...] - w_top], axis=0).astype(BF16)
+
+    def across(v):
+        return lax.dot_general(w_both, v, (((1,), (1,)), ((), ())), preferred_element_type=F32)
+
     parts = []
     for j in range(4):
         xj = xs[pl.ds(j, 128, stride=4), :]
-        pj = lax.dot_general(bproj[...], xj, (((1,), (1,)), ((), ())), precision=lax.Precision.HIGHEST,
-                             preferred_element_type=F32)
-        parts.append(pj + terms[j])
+        top = xj.astype(BF16)
+        rest = (xj - top.astype(F32)).astype(BF16)
+        pj = across(top) + across(rest)
+        parts.append(pj[:8] + pj[8:] + terms[j])
     mine[...] = jnp.concatenate(parts, axis=0).astype(BF16)
     zbuf[g] = mine[...]
     l_hom.wait()
@@ -130,9 +141,10 @@
     with jax.named_scope("barrier"):
         pl.semaphore_wait(barrier, 25)
 
-    def z_copy(p):
-        to = lax.rem(g + p, 16)
-        return remote(mine, zbuf.at[g], z_s, z_r.at[lax.div(z, 4)], far_id(to))
+    def z_copy(n):
+        zz = lax.rem(lax.div(z, 4) + n[0], 2) * 4 + lax.rem(z + n[1], 4)
+        device = {"dap_0": zz, "dap_1": lax.rem(y + n[2], 2)}
+        return remote(mine, zbuf.at[g], z_s, z_r.at[lax.div(z, 4)], device)
 
     def hom_copy(p):
         to = lax.rem(seq + p, 4)
@@ -146,21 +158,25 @@
         to = lax.rem(seq + p, 4)
         return remote(mrow.at[seq], mrow.at[seq], mrow_s, mrow_r, {"seq": to})
 
-    def mz_copy(p):
-        to = lax.rem(g + p, 16)
-        return remote(mzb.at[g], mzb.at[g], mz_s, mz_r, far_id(to))
-
-    def mp_copy(p):
-        to = lax.rem(q + p, 8)
-        return remote(mzb, mcol.at[q], mp_s, mp_r, near_id(to))
+    def mz_copy(n):
+        to, device = far(n)
+        return remote(mzb.at[g], mzb.at[g], mz_s, mz_r, device)
+
+    def mp_copy(n):
+        to, device = near(n)
+        return remote(mzb, mcol.at[q], mp_s, mp_r, device)
 
     def drain(ref, sem):
         pltpu.make_async_copy(ref, ref, sem).wait()
 
-    pl.loop(1, 16)(lambda p: z_copy(p).start())
-    pl.loop(1, 4)(lambda p: hom_copy(p).start())
-    pl.loop(1, 16)(lambda p: mz_copy(p).start())
-    pl.loop(1, 4)(lambda p: mrow_copy(p).start())
+    for n in HALVES:
+        z_copy(n).start()
+    for p in (2, 1, 3):
+        mrow_copy(p).start()
+    for p in (2, 1, 3):
+        hom_copy(p).start()
+    for n in FAR:
+        mz_copy(n).start()
 
     def transposed(v):
         return v.astype(BF16).T
@@ -181,8 +197,10 @@
         rows = pl.ds(pl.multiple_of(lax.rem(b, 2) * 16, 16), 16)
         ref[lax.div(b, 2), :, rows, :] = v.reshape(8, 16, v.shape[-1])
 
-    def block_scores(b, keys, values):
-        place(scores, b, mm(keys.astype(BF16), qbd[...]))
+    def block_scores(b, s, values):
+        seen = mm(order, jnp.broadcast_to(mrow[b].astype(F32), (128, 128)).T.astype(BF16)) > 0.0
+        s = [jnp.where(seen, s[:, h * 128:(h + 1) * 128] * SCALE, -1e30) for h in range(HEADS)]
+        place(scores, b, jnp.concatenate(s, axis=1))
         place(vrow, b, values)
 
     l_wh.wait()
@@ -193,21 +211,28 @@
         spread_queries(transposed(qg[:, :WIDE]))
         gt[...] = transposed(qg[:, 3 * WIDE:]).astype(F32)
         kv = mm(ordered(normed), wh[:, WIDE:3 * WIDE])
-        block_scores(seq, kv[:, :WIDE], kv[:, WIDE:])
-
-    def neighbour_block(p):
-        b = lax.rem(seq + p, 4)
-        with jax.named_scope(f"hom{p}"):
-            hom_recv(p).wait_recv()
-        kv = mm(ordered(layer_norm(homall[b].astype(F32)).astype(BF16)), wh[:, WIDE:3 * WIDE])
-        block_scores(b, kv[:, :WIDE], kv[:, WIDE:])
+        block_scores(seq, mm(kv[:, :WIDE].astype(BF16), qbd[...]), kv[:, WIDE:])
+
+    def neighbour_blocks():
+        drain(mrow.at[pl.ds(0, 3)], mrow_r)
+        blocks = [lax.rem(seq + p, 4) for p in (1, 3, 2)]
+        for p in (1, 3, 2):
+            with jax.named_scope(f"hom{p}"):
+                hom_recv(p).wait_recv()
+        with jax.named_scope("nb"):
+            normed = [ordered(layer_norm(homall[b].astype(F32)).astype(BF16)) for b in blocks]
+            kv = mm(jnp.concatenate(normed, axis=0), wh[:, WIDE:3 * WIDE])
+            s = mm(kv[:, :WIDE].astype(BF16), qbd[...])
+            for n, b in enumerate(blocks):
+                block_scores(b, s[n * 128:(n + 1) * 128], kv[n * 128:(n + 1) * 128, WIDE:])
+            vt[...] = vrow[...].reshape(512, WIDE).astype(BF16).T
 
     partner = {"dap_3": 1 - c}
 
-    def wave_copy(e, p):
-        to = lax.rem(q + p, 8)
-        half = lax.rem(to, 2)
-        return remote(pack.at[e, half], biasall.at[half, e, q], wave_s.at[e], wave_r.at[e], near_id(to))
+    def wave_copy(e, n):
+        to, device = near(n)
+        half = device["dap_3"]
+        return remote(pack.at[e, half], biasall.at[half, e, q], wave_s.at[e], wave_r.at[e], device)
 
     first = lax.div(z, 4)
     second = 1 - first
@@ -219,7 +244,8 @@
         for h in range(HEADS):
             pack[e, h // 4, :, (h % 4) * 128:(h % 4 + 1) * 128] = xs[pl.ds(h, 32, stride=8), :].astype(BF16)
         biasall[c, e, q] = pack[e, c]
-        pl.loop(1, 8)(lambda p: wave_copy(e, p).start())
+        for n in NEAR:
+            wave_copy(e, n).start()
 
     def hand_over(e, n):
         with jax.named_scope(f"wave{n}"):
@@ -228,21 +254,8 @@
 
     wave_send(first, 7)
     wave_send(second, 8)
-    with jax.named_scope("nb1"):
-        neighbour_block(1)
-    with jax.named_scope("nb3"):
-        neighbour_block(3)
     hand_over(first, 0)
-    with jax.named_scope("nb2"):
-        neighbour_block(2)
-    with jax.named_scope("mask"):
-        vt[...] = vrow[...].reshape(512, WIDE).astype(BF16).T
-        drain(mrow.at[pl.ds(0, 3)], mrow_r)
-        for b in range(4):
-            place(keep, b, mm(order, jnp.broadcast_to(mrow[b].astype(F32), (128, 128)).T.astype(BF16)))
-        drain(mzb.at[pl.ds(0, 15)], mz_r)
-    pl.loop(1, 8)(lambda p: mp_copy(p).start())
-    mcol[q] = mzb[...]
+    neighbour_blocks()
     hand_over(second, 1)
 
     def softmax_out(s, vth):
@@ -255,9 +268,8 @@
         head = half * 4 + h
         lanes = pl.ds(pl.multiple_of(head * 128, 128), 128)
         rows = pl.ds(pl.multiple_of(head * 32, 32), 32)
-        s = scores[:, :, :, lanes].reshape(512, 128) * SCALE
+        s = scores[:, :, :, lanes].reshape(512, 128)
         s = s + biasall[half, :, :, :, h * 128:(h + 1) * 128].reshape(512, 128).astype(F32)
-        s = jnp.where(keep[...].reshape(512, 128) > 0.0, s, -1000000000.0)
         ot[rows, :] = softmax_out(s, vt[rows, :])
 
     with jax.named_scope("rowattn"):
@@ -269,9 +281,31 @@
         for h in range(4):
             row_head(1 - c, h)
 
-    def split(v):
-        fs[:128, :] = v[:, :128].astype(F32)
-        fs[128:, :] = v[:, 128:].astype(F32)
+    def pairs(v):
+        fs[pl.ds(0, 128, stride=2), :] = v[:, :128]
+        fs[pl.ds(1, 128, stride=2), :] = v[:, 128:]
+        return fs[...].astype(BF16).reshape(128, 2, 128)
+
+    def unpaired(v):
+        fs[...] = v.reshape(256, 128).astype(F32)
+        return jnp.concatenate([fs[pl.ds(0, 128, stride=2), :], fs[pl.ds(1, 128, stride=2), :]], axis=1)
+
+    mine_row = q * 16 + g
+
+    def exchange(copy):
+        def rest(dz, dims):
+            for dx, dy, dc in dims:
+                to_g = lax.rem(z + dz, 8) * 2 + lax.rem(y + dy, 2)
+                to_q = lax.rem(x + dx, 4) * 2 + lax.rem(c + dc, 2)
+                copy(to_g, to_q, {
+                    "dap_0": lax.rem(z + dz, 8), "dap_1": lax.rem(y + dy, 2),
+                    "dap_2": lax.rem(x + dx, 4), "dap_3": lax.rem(c + dc, 2)}).start()
+
+        @pl.loop(0, 7)
+        def _(n):
+            rest(4 + lax.div(n + 1, 2) * (1 - 2 * lax.rem(n, 2)), ALL)
+
+        rest(0, ALL[:-1])
 
     def gated_project(w):
         g = (jax.nn.sigmoid(gt[...]) * ot[...]).astype(BF16)
@@ -279,40 +313,29 @@
 
     with jax.named_scope("rowproj"):
         l_rest[0].wait()
-        one = (homall[seq].astype(F32) + gated_project(ph[...])).astype(BF16).astype(F32)
-        a1s[...] = one.reshape(16, 8, WIDE).astype(BF16)
-        a1[g] = a1s[g]
-
-    def a1_copy(p):
-        to = lax.rem(g + p, 16)
-        return remote(a1s.at[to], a1.at[g], a1_s, a1_r, far_id(to))
-
-    pl.loop(1, 16)(lambda p: a1_copy(p).start())
-    with jax.named_scope("waita1"):
-        drain(a1.at[pl.ds(0, 15)], a1_r)
-
-    split(a1[...].astype(F32).reshape(128, WIDE))
-    for n in range(8):
-        for t in range(2):
-            a2s[n, :, t * 128:(t + 1) * 128] = fs[pl.ds(t * 128 + n, 16, stride=8), :].astype(BF16)
-    a2[q] = a2s[q]
-
-    def a2_copy(p):
-        to = lax.rem(q + p, 8)
-        return remote(a2s.at[to], a2.at[q], a2_s, a2_r, near_id(to))
-
-    pl.loop(1, 8)(lambda p: a2_copy(p).start())
+        one = homall[seq].astype(F32) + gated_project(ph[...])
+        a1s[...] = pairs(one)
+        a1[mine_row] = a1s[dap]
+
+    def a1_copy(to_g, to_q, device):
+        return remote(a1s.at[to_g * 8 + to_q], a1.at[mine_row], a1_s, a1_r, device)
+
+    exchange(a1_copy)
+    drain(mzb.at[pl.ds(0, 15)], mz_r)
+    for n in NEAR:
+        mp_copy(n).start()
+    mcol[q] = mzb[...]
     for ld in l_rest[1:]:
         ld.wait()
     with jax.named_scope("keepc"):
         drain(mcol.at[pl.ds(0, 7)], mp_r)
         pick = (ri == dap).astype(BF16)
         keepc[...] = mm(mcol[...].reshape(128, 128).astype(F32).astype(BF16), pick)
-    with jax.named_scope("waita2"):
-        drain(a2.at[pl.ds(0, 7)], a2_r)
+    with jax.named_scope("waita1"):
+        drain(a1.at[pl.ds(0, 127)], a1_r)
 
     with jax.named_scope("colattn"):
-        col = a2[...].reshape(128, WIDE).astype(F32)
+        col = unpaired(a1[...])
         qkvg = mm(layer_norm(col).astype(BF16), wc[...])
         spread_queries(transposed(qkvg[:, :WIDE]))
         gt[...] = transposed(qkvg[:, 3 * WIDE:]).astype(F32)
@@ -325,43 +348,27 @@
         two = col + gated_project(pv[...])
         inner = jnp.maximum(mm(layer_norm(two).astype(BF16), ex[...]), 0.0).astype(BF16)
         done = two + mm(inner, co[...])
-        b1s[...] = done.astype(BF16).reshape(8, 16, WIDE)
-        b1[q] = b1s[q]
-
-    def b1_copy(p):
-        to = lax.rem(q + p, 8)
-        return remote(b1s.at[to], b1.at[q], b1_s, b1_r, near_id(to))
-
-    pl.loop(1, 8)(lambda p: b1_copy(p).start())
-    with jax.named_scope("waitb1"):
-        drain(b1.at[pl.ds(0, 7)], b1_r)
-    split(b1[...].reshape(128, WIDE))
-    for n in range(16):
-        for t in range(2):
-            b2s[n, :, t * 128:(t + 1) * 128] = fs[pl.ds(t * 128 + n, 8, stride=16), :].astype(BF16)
-    b2[g] = b2s[g]
-
-    def b2_copy(p):
-        to = lax.rem(g + p, 16)
-        return remote(b2s.at[to], b2.at[g], b2_s, b2_r, far_id(to))
-
-    pl.loop(1, 16)(lambda p: b2_copy(p).start())
+        b1s[...] = pairs(done)
+        b2[dap] = b1s[mine_row]
+
+    def b2_copy(to_g, to_q, device):
+        return remote(b1s.at[to_q * 16 + to_g], b2.at[dap], b2_s, b2_r, device)
+
+    exchange(b2_copy)
 
     drain(zbuf.at[pl.ds(0, 15)], z_s)
     for e in range(2):
         drain(biasall.at[0, 0, pl.ds(0, 7)], wave_s.at[e])
     drain(mcol.at[pl.ds(0, 7)], mp_s)
-    drain(a1.at[pl.ds(0, 15)], a1_s)
-    drain(a2.at[pl.ds(0, 7)], a2_s)
-    drain(b1.at[pl.ds(0, 7)], b1_s)
+    drain(a1.at[pl.ds(0, 127)], a1_s)
     drain(mzb.at[pl.ds(0, 15)], mz_s)
     drain(homall.at[pl.ds(0, 3)], hom_s)
     drain(mrow.at[pl.ds(0, 3)], mrow_s)
     drain(biasall.at[0], part_s)
     with jax.named_scope("waitb2"):
-        drain(b2.at[pl.ds(0, 15)], b2_r)
-    drain(b2.at[pl.ds(0, 15)], b2_s)
-    out[...] = b2[...].astype(F32).reshape(128, WIDE).astype(BF16)
+        drain(b2.at[pl.ds(0, 127)], b2_r)
+    drain(b2.at[pl.ds(0, 127)], b2_s)
+    out[...] = unpaired(b2[...]).astype(BF16)
 
 
 def body(
@@ -398,7 +405,6 @@
             pltpu.VMEM((4, 1, 128), jnp.int32),
             pltpu.VMEM((16, 1, 128), jnp.int32),
             pltpu.VMEM((8, 16, 1, 128), jnp.int32),
-            pltpu.VMEM((2, 8, 32, 128), F32),
             pltpu.VMEM((128, 128), F32),
             pltpu.VMEM((WIDE, 1024), BF16),
             pltpu.VMEM((2, 8, 32, WIDE), F32),
@@ -406,17 +412,13 @@
             pltpu.VMEM((2, 8, 32, 1024), F32),
             pltpu.VMEM((WIDE, 128), F32),
             pltpu.VMEM((WIDE, 128), F32),
-            pltpu.VMEM((16, 8, WIDE), BF16),
-            pltpu.VMEM((16, 8, WIDE), BF16),
-            pltpu.VMEM((8, 16, WIDE), BF16),
-            pltpu.VMEM((8, 16, WIDE), BF16),
-            pltpu.VMEM((8, 16, WIDE), BF16),
-            pltpu.VMEM((8, 16, WIDE), BF16),
-            pltpu.VMEM((16, 8, WIDE), BF16),
-            pltpu.VMEM((16, 8, WIDE), BF16),
+            pltpu.VMEM((128, 2, 128), BF16),
+            pltpu.VMEM((128, 2, 128), BF16),
+            pltpu.VMEM((128, 2, 128), BF16),
+            pltpu.VMEM((128, 2, 128), BF16),
             pltpu.VMEM((256, 128), F32),
             dma((13,)), dma, dma((2,)), dma, dma((4,)), dma, dma, dma, dma, dma, dma,
-            dma((2,)), dma((2,)), dma, dma, dma, dma, dma, dma, dma, dma, dma, dma,
+            dma((2,)), dma((2,)), dma, dma, dma, dma, dma, dma,
         ],
         compiler_params=pltpu.CompilerParams(collective_id=0, has_side_effects=True),
     )(

time: 50 us -> 44.5 us (0.89)
  Pallas kernels: 49.3 us -> 43.8 us
    pallas_call x1, Pallas kernels: 49.3 us -> 43.8 us  [body(): pl.pallas_call(kernel, name='msa_block', out_shape=pltpu.VMEM((128, WIDE)...]
where the time goes in v4:
time: 44.5 us; the launch traced here: 44.4 us
  Pallas kernels  43.8 us (98%)
  local copies, waits for them, and re-layouts  0.63 us (1%)
    pallas_call x1, Pallas kernels, body(): pl.pallas_call(kernel, name='msa_block', out_shape=pltpu.VMEM((128, WIDE)...  43.8 us

profile of v4, /device:TPU:1, one launch (start us, length us, event | category | flops | bytes accessed | tf_op | source)
XLA Modules:
  0.0 44.4 jit_solution(13483327940458831390)
XLA Ops:
  0.0 43.8 %msa_block.1 = bf16[128,256]{1,0:T(8,128)(2,1)S(1)} custom-call(bf16[128,256]{1,0:T(8,128)(2,1)} %bitcast.7, bf16[512,128]{1,0:T(8,128)(2,1)} %bitcast.6, s32[1,128]{1,0:T(1,128)} %mask_h.1, s32[4,128]{1,0:T(4,128)} %bitcast.9, f32[8,128]{1,0:T(8,128)} %bitcast.8, f32[2,8]{1,0:T(2,128)} %cbias_h.1, bf16[256,1024]{1,0:T(8,128)(2,1)} %wh_h.1, ...), custom_call_target="tpu_custom_call" | custom-call | tf_op jit(solution)/shard_map/msa_block/pallas_call | solution.py:382
  43.8 0.6 %copy.14 = bf16[1,128,256]{2,1,0:T(8,128)(2,1)} copy(bf16[1,128,256]{2,1,0:T(8,128)(2,1)S(1)} %bitcast.5) | data formatting | bytes 131072

commit v5 on v4

--- a/solution.py
+++ b/solution.py
@@ -29,6 +29,7 @@
 
 FAR = tuple((dz, dy) for dz in (4, 3, 5, 2, 6, 1, 7, 0) for dy in (1, 0) if dz or dy)
 HALVES = tuple((o, i, dy) for o in range(2) for i in (1, 3, 2, 0) for dy in range(2) if o or i or dy)
+WAVE = tuple((dx, core) for core in range(2) for dx in (2, 1, 3)) + ((0, 0),)
 ALL = tuple((dx, dy, dc) for dx in (2, 1, 3, 0) for dy in (1, 0) for dc in (1, 0))
 NEAR = tuple((dx, dc) for dx in (2, 1, 3, 0) for dc in (1, 0) if dx or dc)
 
@@ -38,7 +39,7 @@
     out,
     pair, chain, bproj, cbias, wh, ph, wc, pv, ex, co,
     xs, mine, zbuf, pack, biasall, homall, mrow, mzb, mcol, keepc,
-    qbd, vrow, vt, scores, ot, gt,
+    qbd, vrow, vt, scores, top, total, ot, gt,
     a1s, a1, b1s, b2, fs,
     lsem, z_s, z_r, hom_s, hom_r, mrow_s, mrow_r, mp_s, mp_r, mz_s, mz_r,
     wave_s, wave_r, part_s, part_r, a1_s, a1_r, b2_s, b2_r,
@@ -65,8 +66,9 @@
     l_wh = local(7, wh_h, wh)
     l_rest = [local(8 + n, a, b) for n, (a, b) in enumerate(
         ((ph_h, ph), (wc_h, wc), (pv_h, pv), (ex_h, ex), (co_h, co)))]
-    for ld in (l_pair, l_chain, l_cbias, l_bproj):
-        ld.start()
+    with jax.named_scope("start"):
+        for ld in (l_pair, l_chain, l_cbias, l_bproj):
+            ld.start()
 
     def remote(src, dst, ss, rs, device):
         return pltpu.make_async_remote_copy(
@@ -127,9 +129,9 @@
     parts = []
     for j in range(4):
         xj = xs[pl.ds(j, 128, stride=4), :]
-        top = xj.astype(BF16)
-        rest = (xj - top.astype(F32)).astype(BF16)
-        pj = across(top) + across(rest)
+        high = xj.astype(BF16)
+        low = (xj - high.astype(F32)).astype(BF16)
+        pj = across(high) + across(low)
         parts.append(pj[:8] + pj[8:] + terms[j])
     mine[...] = jnp.concatenate(parts, axis=0).astype(BF16)
     zbuf[g] = mine[...]
@@ -230,9 +232,9 @@
     partner = {"dap_3": 1 - c}
 
     def wave_copy(e, n):
-        to, device = near(n)
-        half = device["dap_3"]
-        return remote(pack.at[e, half], biasall.at[half, e, q], wave_s.at[e], wave_r.at[e], device)
+        xx, half = lax.rem(x + n[0], 4), (1 - c if n[0] == 0 else n[1])
+        device = {"dap_2": xx, "dap_3": half}
+        return remote(pack.at[e, half], biasall.at[half, e, q], wave_s.at[e], wave_r.at[e, q], device)
 
     first = lax.div(z, 4)
     second = 1 - first
@@ -244,42 +246,82 @@
         for h in range(HEADS):
             pack[e, h // 4, :, (h % 4) * 128:(h % 4 + 1) * 128] = xs[pl.ds(h, 32, stride=8), :].astype(BF16)
         biasall[c, e, q] = pack[e, c]
-        for n in NEAR:
+        for n in WAVE:
             wave_copy(e, n).start()
 
+    def pass_on(e, block):
+        remote(biasall.at[c, e, block], biasall.at[c, e, block], part_s.at[e], part_r.at[e], partner).start()
+
     def hand_over(e, n):
+        pass_on(e, q)
         with jax.named_scope(f"wave{n}"):
-            drain(biasall.at[0, 0, pl.ds(0, 7)], wave_r.at[e])
-        remote(biasall.at[c, e], biasall.at[c, e], part_s, part_r, partner).start()
+            for m in reversed(NEAR):
+                block = near(m)[0]
+                drain(biasall.at[0, 0, 0], wave_r.at[e, block])
+                pass_on(e, block)
 
     wave_send(first, 7)
     wave_send(second, 8)
     hand_over(first, 0)
     neighbour_blocks()
+
+    def half_scores(e, half, h):
+        lanes = pl.ds(pl.multiple_of((half * 4 + h) * 128, 128), 128)
+        s = scores[e, :, :, lanes].reshape(256, 128)
+        return s + biasall[half, e, :, :, h * 128:(h + 1) * 128].reshape(256, 128).astype(F32)
+
+    def first_half(half):
+        for h in range(4):
+            s = half_scores(first, half, h)
+            m = jnp.max(s, axis=0, keepdims=True)
+            e = jnp.exp(s - m)
+            scores[first, :, :, pl.ds(pl.multiple_of((half * 4 + h) * 128, 128), 128)] = e.reshape(8, 32, 128)
+            top[half * 4 + h] = m
+            total[half * 4 + h] = jnp.sum(e, axis=0, keepdims=True)
+
+    def second_half(half):
+        for h in range(4):
+            head = half * 4 + h
+            s = half_scores(second, half, h)
+            m = jnp.maximum(top[head], jnp.max(s, axis=0, keepdims=True))
+            e = jnp.exp(s - m)
+            before = jnp.exp(top[head] - m)
+            share = 1.0 / (total[head] * before + jnp.sum(e, axis=0, keepdims=True))
+            old = scores[first, :, :, pl.ds(pl.multiple_of(head * 128, 128), 128)].reshape(256, 128)
+            rows = pl.ds(pl.multiple_of(head * 32, 32), 32)
+            ot[rows, :] = (
+                mm(vt[rows, pl.ds(pl.multiple_of(first * 256, 256), 256)], (old * (before * share)).astype(BF16))
+                + mm(vt[rows, pl.ds(pl.multiple_of(second * 256, 256), 256)], (e * share).astype(BF16)))
+
+    with jax.named_scope("half1"):
+        first_half(c)
+
+    def partner_first_half():
+        drain(biasall.at[1 - c, 0], part_r.at[first])
+        first_half(1 - c)
+
+    @pl.when(c == 0)
+    def _():
+        partner_first_half()
+
     hand_over(second, 1)
+
+    @pl.when(c == 1)
+    def _():
+        partner_first_half()
+
+    with jax.named_scope("rowattn"):
+        second_half(c)
+    with jax.named_scope("partner"):
+        drain(biasall.at[1 - c, 0], part_r.at[second])
+    with jax.named_scope("rowattn2"):
+        second_half(1 - c)
 
     def softmax_out(s, vth):
         m = jnp.max(s, axis=0, keepdims=True)
         e = jnp.exp(s - m)
         w = (e * (1.0 / jnp.sum(e, axis=0, keepdims=True))).astype(BF16)
         return mm(vth, w)
-
-    def row_head(half, h):
-        head = half * 4 + h
-        lanes = pl.ds(pl.multiple_of(head * 128, 128), 128)
-        rows = pl.ds(pl.multiple_of(head * 32, 32), 32)
-        s = scores[:, :, :, lanes].reshape(512, 128)
-        s = s + biasall[half, :, :, :, h * 128:(h + 1) * 128].reshape(512, 128).astype(F32)
-        ot[rows, :] = softmax_out(s, vt[rows, :])
-
-    with jax.named_scope("rowattn"):
-        for h in range(4):
-            row_head(c, h)
-    with jax.named_scope("partner"):
-        drain(biasall.at[1 - c], part_r)
-    with jax.named_scope("rowattn2"):
-        for h in range(4):
-            row_head(1 - c, h)
 
     def pairs(v):
         fs[pl.ds(0, 128, stride=2), :] = v[:, :128]
@@ -364,7 +406,8 @@
     drain(mzb.at[pl.ds(0, 15)], mz_s)
     drain(homall.at[pl.ds(0, 3)], hom_s)
     drain(mrow.at[pl.ds(0, 3)], mrow_s)
-    drain(biasall.at[0], part_s)
+    for e in range(2):
+        drain(biasall.at[0, 0], part_s.at[e])
     with jax.named_scope("waitb2"):
         drain(b2.at[pl.ds(0, 127)], b2_r)
     drain(b2.at[pl.ds(0, 127)], b2_s)
@@ -410,6 +453,8 @@
             pltpu.VMEM((2, 8, 32, WIDE), F32),
             pltpu.VMEM((WIDE, 512), BF16),
             pltpu.VMEM((2, 8, 32, 1024), F32),
+            pltpu.VMEM((8, 1, 128), F32),
+            pltpu.VMEM((8, 1, 128), F32),
             pltpu.VMEM((WIDE, 128), F32),
             pltpu.VMEM((WIDE, 128), F32),
             pltpu.VMEM((128, 2, 128), BF16),
@@ -418,7 +463,7 @@
             pltpu.VMEM((128, 2, 128), BF16),
             pltpu.VMEM((256, 128), F32),
             dma((13,)), dma, dma((2,)), dma, dma((4,)), dma, dma, dma, dma, dma, dma,
-            dma((2,)), dma((2,)), dma, dma, dma, dma, dma, dma,
+            dma((2,)), dma((2, 8)), dma((2,)), dma((2,)), dma, dma, dma, dma,
         ],
         compiler_params=pltpu.CompilerParams(collective_id=0, has_side_effects=True),
     )(

time: 44.5 us -> 44 us (0.989)
  Pallas kernels: 43.8 us -> 43.3 us
    pallas_call x1, Pallas kernels: 43.8 us -> 43.3 us  [body(): pl.pallas_call(kernel, name='msa_block', out_shape=pltpu.VMEM((128, WIDE)...]
where the time goes in v5:
time: 44 us; the launch traced here: 43.9 us
  Pallas kernels  43.3 us (98%)
  local copies, waits for them, and re-layouts  0.63 us (1%)
    pallas_call x1, Pallas kernels, body(): pl.pallas_call(kernel, name='msa_block', out_shape=pltpu.VMEM((128, WIDE)...  43.3 us

profile of v5, /device:TPU:1, one launch (start us, length us, event | category | flops | bytes accessed | tf_op | source)
XLA Modules:
  0.0 43.9 jit_solution(6323171165083101828)
XLA Ops:
  0.0 43.3 %msa_block.1 = bf16[128,256]{1,0:T(8,128)(2,1)S(1)} custom-call(bf16[128,256]{1,0:T(8,128)(2,1)} %bitcast.7, bf16[512,128]{1,0:T(8,128)(2,1)} %bitcast.6, s32[1,128]{1,0:T(1,128)} %mask_h.1, s32[4,128]{1,0:T(4,128)} %bitcast.9, f32[8,128]{1,0:T(8,128)} %bitcast.8, f32[2,8]{1,0:T(2,128)} %cbias_h.1, bf16[256,1024]{1,0:T(8,128)(2,1)} %wh_h.1, ...), custom_call_target="tpu_custom_call" | custom-call | tf_op jit(solution)/shard_map/msa_block/pallas_call | solution.py:425
  43.3 0.6 %copy.14 = bf16[1,128,256]{2,1,0:T(8,128)(2,1)} copy(bf16[1,128,256]{2,1,0:T(8,128)(2,1)S(1)} %bitcast.5) | data formatting | bytes 131072

commit v6 on v5

--- a/solution.py
+++ b/solution.py
@@ -28,7 +28,7 @@
 
 
 FAR = tuple((dz, dy) for dz in (4, 3, 5, 2, 6, 1, 7, 0) for dy in (1, 0) if dz or dy)
-HALVES = tuple((o, i, dy) for o in range(2) for i in (1, 3, 2, 0) for dy in range(2) if o or i or dy)
+PAIRS = tuple((o, i, dy) for o in (0, 1, 3, 2) for i in (1, 0) for dy in range(2) if o or i or dy)
 WAVE = tuple((dx, core) for core in range(2) for dx in (2, 1, 3)) + ((0, 0),)
 ALL = tuple((dx, dy, dc) for dx in (2, 1, 3, 0) for dy in (1, 0) for dc in (1, 0))
 NEAR = tuple((dx, dc) for dx in (2, 1, 3, 0) for dc in (1, 0) if dx or dc)
@@ -42,7 +42,7 @@
     qbd, vrow, vt, scores, top, total, ot, gt,
     a1s, a1, b1s, b2, fs,
     lsem, z_s, z_r, hom_s, hom_r, mrow_s, mrow_r, mp_s, mp_r, mz_s, mz_r,
-    wave_s, wave_r, part_s, part_r, a1_s, a1_r, b2_s, b2_r,
+    wave_s, wave_r, last_r, part_s, part_r, a1_s, a1_r, b2_s, b2_r,
 ):
     z = lax.axis_index("dap_0")
     y = lax.axis_index("dap_1")
@@ -144,9 +144,9 @@
         pl.semaphore_wait(barrier, 25)
 
     def z_copy(n):
-        zz = lax.rem(lax.div(z, 4) + n[0], 2) * 4 + lax.rem(z + n[1], 4)
+        zz = lax.rem(lax.div(z, 2) + n[0], 4) * 2 + lax.rem(z + n[1], 2)
         device = {"dap_0": zz, "dap_1": lax.rem(y + n[2], 2)}
-        return remote(mine, zbuf.at[g], z_s, z_r.at[lax.div(z, 4)], device)
+        return remote(mine, zbuf.at[g], z_s, z_r.at[lax.div(z, 2)], device)
 
     def hom_copy(p):
         to = lax.rem(seq + p, 4)
@@ -171,7 +171,7 @@
     def drain(ref, sem):
         pltpu.make_async_copy(ref, ref, sem).wait()
 
-    for n in HALVES:
+    for n in PAIRS:
         z_copy(n).start()
     for p in (2, 1, 3):
         mrow_copy(p).start()
@@ -196,8 +196,7 @@
         return mm(order, v).astype(BF16)
 
     def place(ref, b, v):
-        rows = pl.ds(pl.multiple_of(lax.rem(b, 2) * 16, 16), 16)
-        ref[lax.div(b, 2), :, rows, :] = v.reshape(8, 16, v.shape[-1])
+        ref[b] = v.reshape(8, 16, v.shape[-1])
 
     def block_scores(b, s, values):
         seen = mm(order, jnp.broadcast_to(mrow[b].astype(F32), (128, 128)).T.astype(BF16)) > 0.0
@@ -231,91 +230,95 @@
 
     partner = {"dap_3": 1 - c}
 
-    def wave_copy(e, n):
-        xx, half = lax.rem(x + n[0], 4), (1 - c if n[0] == 0 else n[1])
+    def wave_copy(n, to):
+        e = waves[n]
+        xx, half = lax.rem(x + to[0], 4), (1 - c if to[0] == 0 else to[1])
         device = {"dap_2": xx, "dap_3": half}
-        return remote(pack.at[e, half], biasall.at[half, e, q], wave_s.at[e], wave_r.at[e, q], device)
-
-    first = lax.div(z, 4)
-    second = 1 - first
-
-    def wave_send(e, count):
-        with jax.named_scope(f"zwait{count}"):
+        arrived = wave_r.at[n] if n < 3 else last_r.at[q]
+        return remote(pack.at[e, half], biasall.at[half, e, q], wave_s, arrived, device)
+
+    waves = [lax.rem(lax.div(z, 2) + o, 4) for o in (0, 1, 3, 2)]
+
+    def wave_send(n, count):
+        e = waves[n]
+        with jax.named_scope(f"zwait{n}"):
             drain(zbuf.at[pl.ds(0, count)], z_r.at[e])
-        xs[:256, :] = zbuf[pl.ds(e * 8, 8)].reshape(256, 128).astype(F32)
+        xs[:128, :] = zbuf[pl.ds(e * 4, 4)].reshape(128, 128).astype(F32)
         for h in range(HEADS):
-            pack[e, h // 4, :, (h % 4) * 128:(h % 4 + 1) * 128] = xs[pl.ds(h, 32, stride=8), :].astype(BF16)
+            pack[e, h // 4, :, (h % 4) * 128:(h % 4 + 1) * 128] = xs[pl.ds(h, 16, stride=8), :].astype(BF16)
         biasall[c, e, q] = pack[e, c]
-        for n in WAVE:
-            wave_copy(e, n).start()
-
-    def pass_on(e, block):
-        remote(biasall.at[c, e, block], biasall.at[c, e, block], part_s.at[e], part_r.at[e], partner).start()
-
-    def hand_over(e, n):
-        pass_on(e, q)
+        for to in WAVE:
+            wave_copy(n, to).start()
+
+    def pass_on(n, ref):
+        remote(ref, ref, part_s, part_r.at[n], partner).start()
+
+    def hand_over(n):
+        e = waves[n]
         with jax.named_scope(f"wave{n}"):
-            for m in reversed(NEAR):
-                block = near(m)[0]
-                drain(biasall.at[0, 0, 0], wave_r.at[e, block])
-                pass_on(e, block)
-
-    wave_send(first, 7)
-    wave_send(second, 8)
-    hand_over(first, 0)
+            if n < 3:
+                drain(biasall.at[0, 0, pl.ds(0, 7)], wave_r.at[n])
+                pass_on(n, biasall.at[c, e])
+            else:
+                pass_on(n, biasall.at[c, e, q])
+                for m in reversed(NEAR):
+                    block = near(m)[0]
+                    drain(biasall.at[0, 0, 0], last_r.at[block])
+                    pass_on(n, biasall.at[c, e, block])
+
+    wave_send(0, 3)
+    for n in range(1, 4):
+        wave_send(n, 4)
+    hand_over(0)
     neighbour_blocks()
-
-    def half_scores(e, half, h):
+    hand_over(1)
+    hand_over(2)
+
+    def wave_scores(e, half, h):
         lanes = pl.ds(pl.multiple_of((half * 4 + h) * 128, 128), 128)
-        s = scores[e, :, :, lanes].reshape(256, 128)
-        return s + biasall[half, e, :, :, h * 128:(h + 1) * 128].reshape(256, 128).astype(F32)
-
-    def first_half(half):
+        s = scores[e, :, :, lanes].reshape(128, 128)
+        return s + biasall[half, e, :, :, h * 128:(h + 1) * 128].reshape(128, 128).astype(F32)
+
+    def first_part(half):
         for h in range(4):
-            s = half_scores(first, half, h)
-            m = jnp.max(s, axis=0, keepdims=True)
-            e = jnp.exp(s - m)
-            scores[first, :, :, pl.ds(pl.multiple_of((half * 4 + h) * 128, 128), 128)] = e.reshape(8, 32, 128)
+            s = [wave_scores(e, half, h) for e in waves[:3]]
+            m = jnp.max(jnp.maximum(jnp.maximum(s[0], s[1]), s[2]), axis=0, keepdims=True)
+            p = [jnp.exp(v - m) for v in s]
+            for e, v in zip(waves, p):
+                scores[e, :, :, pl.ds(pl.multiple_of((half * 4 + h) * 128, 128), 128)] = v.reshape(8, 16, 128)
             top[half * 4 + h] = m
-            total[half * 4 + h] = jnp.sum(e, axis=0, keepdims=True)
-
-    def second_half(half):
+            total[half * 4 + h] = jnp.sum(p[0] + p[1] + p[2], axis=0, keepdims=True)
+
+    def last_part(half):
         for h in range(4):
             head = half * 4 + h
-            s = half_scores(second, half, h)
+            rows = pl.ds(pl.multiple_of(head * 32, 32), 32)
+            s = wave_scores(waves[3], half, h)
             m = jnp.maximum(top[head], jnp.max(s, axis=0, keepdims=True))
-            e = jnp.exp(s - m)
+            p = jnp.exp(s - m)
             before = jnp.exp(top[head] - m)
-            share = 1.0 / (total[head] * before + jnp.sum(e, axis=0, keepdims=True))
-            old = scores[first, :, :, pl.ds(pl.multiple_of(head * 128, 128), 128)].reshape(256, 128)
-            rows = pl.ds(pl.multiple_of(head * 32, 32), 32)
-            ot[rows, :] = (
-                mm(vt[rows, pl.ds(pl.multiple_of(first * 256, 256), 256)], (old * (before * share)).astype(BF16))
-                + mm(vt[rows, pl.ds(pl.multiple_of(second * 256, 256), 256)], (e * share).astype(BF16)))
+            share = 1.0 / (total[head] * before + jnp.sum(p, axis=0, keepdims=True))
+            lanes = pl.ds(pl.multiple_of(head * 128, 128), 128)
+            parts = [scores[e, :, :, lanes].reshape(128, 128) * (before * share) for e in waves[:3]] + [p * share]
+            ot[rows, :] = sum(
+                mm(vt[rows, pl.ds(pl.multiple_of(e * 128, 128), 128)], v.astype(BF16))
+                for e, v in zip(waves, parts))
 
     with jax.named_scope("half1"):
-        first_half(c)
-
-    def partner_first_half():
-        drain(biasall.at[1 - c, 0], part_r.at[first])
-        first_half(1 - c)
-
-    @pl.when(c == 0)
-    def _():
-        partner_first_half()
-
-    hand_over(second, 1)
-
-    @pl.when(c == 1)
-    def _():
-        partner_first_half()
-
+        first_part(c)
+
+    hand_over(3)
     with jax.named_scope("rowattn"):
-        second_half(c)
+        last_part(c)
+    with jax.named_scope("partner0"):
+        for n in range(3):
+            drain(biasall.at[1 - c, 0], part_r.at[n])
+    with jax.named_scope("half1b"):
+        first_part(1 - c)
     with jax.named_scope("partner"):
-        drain(biasall.at[1 - c, 0], part_r.at[second])
+        drain(biasall.at[1 - c, 0], part_r.at[3])
     with jax.named_scope("rowattn2"):
-        second_half(1 - c)
+        last_part(1 - c)
 
     def softmax_out(s, vth):
         m = jnp.max(s, axis=0, keepdims=True)
@@ -399,15 +402,13 @@
     exchange(b2_copy)
 
     drain(zbuf.at[pl.ds(0, 15)], z_s)
-    for e in range(2):
-        drain(biasall.at[0, 0, pl.ds(0, 7)], wave_s.at[e])
+    drain(wh.at[pl.ds(0, 224)], wave_s)
     drain(mcol.at[pl.ds(0, 7)], mp_s)
     drain(a1.at[pl.ds(0, 127)], a1_s)
     drain(mzb.at[pl.ds(0, 15)], mz_s)
     drain(homall.at[pl.ds(0, 3)], hom_s)
     drain(mrow.at[pl.ds(0, 3)], mrow_s)
-    for e in range(2):
-        drain(biasall.at[0, 0], part_s.at[e])
+    drain(biasall.at[0], part_s)
     with jax.named_scope("waitb2"):
         drain(b2.at[pl.ds(0, 127)], b2_r)
     drain(b2.at[pl.ds(0, 127)], b2_s)
@@ -442,17 +443,17 @@
             pltpu.VMEM((512, 128), F32),
             pltpu.VMEM((32, 128), BF16),
             pltpu.VMEM((16, 32, 128), BF16),
-            pltpu.VMEM((2, 2, 32, 512), BF16),
-            pltpu.VMEM((2, 2, 8, 32, 512), BF16),
+            pltpu.VMEM((4, 2, 16, 512), BF16),
+            pltpu.VMEM((2, 4, 8, 16, 512), BF16),
             pltpu.VMEM((4, 128, WIDE), BF16),
             pltpu.VMEM((4, 1, 128), jnp.int32),
             pltpu.VMEM((16, 1, 128), jnp.int32),
             pltpu.VMEM((8, 16, 1, 128), jnp.int32),
             pltpu.VMEM((128, 128), F32),
             pltpu.VMEM((WIDE, 1024), BF16),
-            pltpu.VMEM((2, 8, 32, WIDE), F32),
+            pltpu.VMEM((4, 8, 16, WIDE), F32),
             pltpu.VMEM((WIDE, 512), BF16),
-            pltpu.VMEM((2, 8, 32, 1024), F32),
+            pltpu.VMEM((4, 8, 16, 1024), F32),
             pltpu.VMEM((8, 1, 128), F32),
             pltpu.VMEM((8, 1, 128), F32),
             pltpu.VMEM((WIDE, 128), F32),
@@ -462,8 +463,8 @@
             pltpu.VMEM((128, 2, 128), BF16),
             pltpu.VMEM((128, 2, 128), BF16),
             pltpu.VMEM((256, 128), F32),
-            dma((13,)), dma, dma((2,)), dma, dma((4,)), dma, dma, dma, dma, dma, dma,
-            dma((2,)), dma((2, 8)), dma((2,)), dma((2,)), dma, dma, dma, dma,
+            dma((13,)), dma, dma((4,)), dma, dma((4,)), dma, dma, dma, dma, dma, dma,
+            dma, dma((3,)), dma((8,)), dma, dma((4,)), dma, dma, dma, dma,
         ],
         compiler_params=pltpu.CompilerParams(collective_id=0, has_side_effects=True),
     )(

time: 44 us -> 43.7 us (level)
  no operation moved by 1% of the time
where the time goes in v6:
time: 43.7 us; the launch traced here: 43.6 us
  Pallas kernels  42.9 us (98%)
  local copies, waits for them, and re-layouts  0.63 us (1%)
    pallas_call x1, Pallas kernels, body(): pl.pallas_call(kernel, name='msa_block', out_shape=pltpu.VMEM((128, WIDE)...  42.9 us

profile of v6, /device:TPU:1, one launch (start us, length us, event | category | flops | bytes accessed | tf_op | source)
XLA Modules:
  0.0 43.6 jit_solution(10856487375565233234)
XLA Ops:
  0.0 42.9 %msa_block.1 = bf16[128,256]{1,0:T(8,128)(2,1)S(1)} custom-call(bf16[128,256]{1,0:T(8,128)(2,1)} %bitcast.7, bf16[512,128]{1,0:T(8,128)(2,1)} %bitcast.6, s32[1,128]{1,0:T(1,128)} %mask_h.1, s32[4,128]{1,0:T(4,128)} %bitcast.9, f32[8,128]{1,0:T(8,128)} %bitcast.8, f32[2,8]{1,0:T(2,128)} %cbias_h.1, bf16[256,1024]{1,0:T(8,128)(2,1)} %wh_h.1, ...), custom_call_target="tpu_custom_call" | custom-call | tf_op jit(solution)/shard_map/msa_block/pallas_call | solution.py:426
  42.9 0.6 %copy.14 = bf16[1,128,256]{2,1,0:T(8,128)(2,1)} copy(bf16[1,128,256]{2,1,0:T(8,128)(2,1)S(1)} %bitcast.5) | data formatting | bytes 131072

commit v7 on v6

--- a/solution.py
+++ b/solution.py
@@ -28,7 +28,7 @@
 
 
 FAR = tuple((dz, dy) for dz in (4, 3, 5, 2, 6, 1, 7, 0) for dy in (1, 0) if dz or dy)
-PAIRS = tuple((o, i, dy) for o in (0, 1, 3, 2) for i in (1, 0) for dy in range(2) if o or i or dy)
+PAIRS = tuple((o, i, dy) for o in range(4) for i in (1, 0) for dy in range(2) if o or i or dy)
 WAVE = tuple((dx, core) for core in range(2) for dx in (2, 1, 3)) + ((0, 0),)
 ALL = tuple((dx, dy, dc) for dx in (2, 1, 3, 0) for dy in (1, 0) for dc in (1, 0))
 NEAR = tuple((dx, dc) for dx in (2, 1, 3, 0) for dc in (1, 0) if dx or dc)
@@ -143,8 +143,12 @@
     with jax.named_scope("barrier"):
         pl.semaphore_wait(barrier, 25)
 
+    pair_z = lax.div(z, 2)
+    other_z = pair_z + 1 - 2 * lax.rem(pair_z, 2)
+    waves = [pair_z, other_z, lax.rem(pair_z + 2, 4), lax.rem(other_z + 2, 4)]
+
     def z_copy(n):
-        zz = lax.rem(lax.div(z, 2) + n[0], 4) * 2 + lax.rem(z + n[1], 2)
+        zz = waves[n[0]] * 2 + lax.rem(z + n[1], 2)
         device = {"dap_0": zz, "dap_1": lax.rem(y + n[2], 2)}
         return remote(mine, zbuf.at[g], z_s, z_r.at[lax.div(z, 2)], device)
 
@@ -236,8 +240,6 @@
         device = {"dap_2": xx, "dap_3": half}
         arrived = wave_r.at[n] if n < 3 else last_r.at[q]
         return remote(pack.at[e, half], biasall.at[half, e, q], wave_s, arrived, device)
-
-    waves = [lax.rem(lax.div(z, 2) + o, 4) for o in (0, 1, 3, 2)]
 
     def wave_send(n, count):
         e = waves[n]

time: 43.7 us -> 43.6 us (level)
  no operation moved by 1% of the time
where the time goes in v7:
time: 43.6 us; the launch traced here: 43.4 us
  Pallas kernels  42.8 us (98%)
  local copies, waits for them, and re-layouts  0.63 us (1%)
    pallas_call x1, Pallas kernels, body(): pl.pallas_call(kernel, name='msa_block', out_shape=pltpu.VMEM((128, WIDE)...  42.8 us

profile of v7, /device:TPU:1, one launch (start us, length us, event | category | flops | bytes accessed | tf_op | source)
XLA Modules:
  0.0 43.4 jit_solution(11056731594016084457)
XLA Ops:
  0.0 42.8 %msa_block.1 = bf16[128,256]{1,0:T(8,128)(2,1)S(1)} custom-call(bf16[128,256]{1,0:T(8,128)(2,1)} %bitcast.7, bf16[512,128]{1,0:T(8,128)(2,1)} %bitcast.6, s32[1,128]{1,0:T(1,128)} %mask_h.1, s32[4,128]{1,0:T(4,128)} %bitcast.9, f32[8,128]{1,0:T(8,128)} %bitcast.8, f32[2,8]{1,0:T(2,128)} %cbias_h.1, bf16[256,1024]{1,0:T(8,128)(2,1)} %wh_h.1, ...), custom_call_target="tpu_custom_call" | custom-call | tf_op jit(solution)/shard_map/msa_block/pallas_call | solution.py:428
  42.8 0.6 %copy.14 = bf16[1,128,256]{2,1,0:T(8,128)(2,1)} copy(bf16[1,128,256]{2,1,0:T(8,128)(2,1)S(1)} %bitcast.5) | data formatting | bytes 131072
